TPU v7x, 1024 devices: a whole 8x8x8 slice. The times are simulated.
1024 devices in a mesh: lon: 256 (over z, y, x_lo), lat: 4 (over x_hi, core).
Axes of the slice: x: 8 (x_hi: 2, x_lo: 4; x = x_hi * 4 + x_lo), y: 8, z: 8, core: 2. Of those that a mesh axis runs over, the one named last changes fastest.
Arguments:
- u_vel: float32 [40, 2048, 2048], P(None, 'lon', 'lat'), may hold values from -6 to 6
- v_vel: float32 [40, 2048, 2048], P(None, 'lon', 'lat'), may hold values from -6 to 6
- thickness: float32 [40], replicated, may hold values from 0.5 to 2
- depth: float32 [2048, 2048], P('lon', 'lat'), may hold values from 0.5 to 2
- sea_mask: int32 [2048, 2048], P('lon', 'lat'), may hold values 0 or 1
- damping: float32 [2048, 2048], P('lon', 'lat'), may hold values from 0.1 to 2
- eta_prev: float32 [2048, 2048], P('lon', 'lat'), may hold values from -6 to 6
Outputs:
- surface: float32 [2048, 2048], P('lon', 'lat')
- residual: float32 [2048, 2048], P('lon', 'lat')
All inputs are finite; a program needn't handle non-finite values. No bound on the sum of `sea_mask` on one device may be relied on, other than what follows from the above.
Results may differ from a plain program's by a relative error of at most 0.0003.
Values sent between devices are 32-bit elements; how exact they have to be, the bound alone decides.
No kernel may reach another device: no remote copies, remote signals or barrier semaphores. Data moves between devices by JAX's collectives and lax.ppermute only.
A program may use at most 32 MiB of HBM per device.

v0:
```python
import functools
import math

import jax
import jax.numpy as jnp
from jax import lax
from jax.sharding import Mesh
from jax.sharding import PartitionSpec as P

LEVELS = 40
ITERS = 3
LAT = ("lat_0", "lat_1")
LON_LAT = ("lon_0", "lon_1", "lon_2", "lat_0", "lat_1")
LON = ("lon_0", "lon_1", "lon_2")


def padded_2(value, sides, width):
    edges = {}
    for axis, dim in sides:
        peers, length = (lax.axis_size(axis), value.shape[dim])
        up = [(i, (i + 1) % peers) for i in range(peers)]
        last = lax.slice_in_dim(value, length - width, length, axis=dim)
        leading = lax.slice_in_dim(value, 0, width, axis=dim)
        edges[dim] = (
            lax.ppermute(last, axis, up),
            lax.ppermute(leading, axis, [(b, a) for a, b in up]),
        )
    done = []
    for _, dim in sides:
        low, high = edges[dim]
        around = [(width, width) if d in done else (0, 0) for d in range(value.ndim)]
        value = jnp.concatenate([jnp.pad(low, around), value, jnp.pad(high, around)], axis=dim)
        done.append(dim)
    return value


def extended_2(block, sides, width):
    for axis, dim in sides:
        count = lax.axis_size(axis)
        forward = [(i, i + 1) for i in range(count - 1)]
        forward.append((count - 1, 0))
        backward = [(target, source) for source, target in forward]
        low = lax.ppermute(
            lax.slice_in_dim(block, block.shape[dim] - width, None, axis=dim), axis, forward
        )
        high = lax.ppermute(lax.slice_in_dim(block, 0, width, axis=dim), axis, backward)
        block = jnp.concatenate([low, block, high], axis=dim)
    return block


def by_axis(value, axes):
    return functools.reduce(lax.psum, axes, value)


def close_walls(extended, width):
    position = lax.axis_index(LAT)
    count = lax.axis_size(LAT)
    total = extended.shape[-1]
    column = lax.broadcasted_iota(jnp.int32, extended.shape, extended.ndim - 1)
    bottom = jnp.logical_and(position == 0, column < width)
    top = jnp.logical_and(position == count - 1, column >= total - width)
    keep = jnp.logical_not(jnp.logical_or(bottom, top)).astype(jnp.float32)
    return extended * keep


def column_sum(thickness, velocity):
    return jnp.einsum("k,kxy->xy", thickness, velocity, precision=lax.Precision.HIGHEST) * (
        1.0 / math.sqrt(LEVELS)
    )


def apply_padded(padded, diag, coef_east, coef_west, coef_north, coef_south):
    field = padded[1:-1, 1:-1]
    result = diag * field - coef_east * padded[2:, 1:-1] - coef_west * padded[:-2, 1:-1]
    return result - coef_north * padded[1:-1, 2:] - coef_south * padded[1:-1, :-2]


def operate(field, diag, coef_east, coef_west, coef_north, coef_south):
    padded = padded_2(field, ((LON, 0), (LAT, 1)), 1)
    return apply_padded(padded, diag, coef_east, coef_west, coef_north, coef_south)


def body(u_vel, v_vel, thickness, depth, sea_mask, damping, eta_prev):
    wet = sea_mask.astype(jnp.float32)
    width = 2
    surface_fields = [depth, wet, damping, eta_prev]
    stacked = jnp.stack(
        [column_sum(thickness, u_vel), column_sum(thickness, v_vel)] + surface_fields, axis=0
    )
    extended = extended_2(stacked, ((LON, 1), (LAT, 2)), width)
    extended = close_walls(extended, width)
    sum_east = extended[0]
    sum_north = extended[1]
    rest = extended[2:]
    depth_ext = rest[0]
    wet_ext = rest[1]
    wet_x = wet_ext[:-1, :] * wet_ext[1:, :]
    face_x = wet_x * 0.5 * (depth_ext[:-1, :] + depth_ext[1:, :])
    flux_x = wet_x * sum_east[:-1, :]
    wet_y = wet_ext[:, :-1] * wet_ext[:, 1:]
    face_y = wet_y * 0.5 * (depth_ext[:, :-1] + depth_ext[:, 1:])
    flux_y = wet_y * sum_north[:, :-1]
    coef_east, coef_west = (face_x[1:, 1:-1], face_x[:-1, 1:-1])
    coef_north, coef_south = (face_y[1:-1, 1:], face_y[1:-1, :-1])
    diverge = flux_x[1:, 1:-1] - flux_x[:-1, 1:-1] + flux_y[1:-1, 1:] - flux_y[1:-1, :-1]
    wet_mid = wet_ext[1:-1, 1:-1]
    damp_mid = rest[2][1:-1, 1:-1]
    rhs_mid = wet_mid * (damp_mid * rest[3][1:-1, 1:-1] - diverge)
    diag_mid = damp_mid + coef_east + coef_west + coef_north + coef_south
    precond_mid = rhs_mid / jnp.where(diag_mid > 0.0, diag_mid, 1.0)
    coef_east, coef_west = (coef_east[1:-1, 1:-1], coef_west[1:-1, 1:-1])
    coef_north, coef_south = (coef_north[1:-1, 1:-1], coef_south[1:-1, 1:-1])
    rhs = rhs_mid[1:-1, 1:-1]
    diag = diag_mid[1:-1, 1:-1]

    def sums(residual, precond, image):
        return (
            by_axis(jnp.sum(residual * precond), LON_LAT),
            by_axis(jnp.sum(image * precond), LON_LAT),
        )

    surface = jnp.zeros_like(rhs)
    residual = rhs
    precond = precond_mid[1:-1, 1:-1]
    image = apply_padded(precond_mid, diag, coef_east, coef_west, coef_north, coef_south)
    gamma_now, delta_now = sums(residual, precond, image)
    step_size = gamma_now / delta_now
    direction, along_dir = (precond, image)
    for sweep in range(ITERS):
        surface = surface + step_size * direction
        residual = residual - step_size * along_dir
        if sweep + 1 < ITERS:
            precond = residual / diag
            image = operate(precond, diag, coef_east, coef_west, coef_north, coef_south)
            gamma_next, delta_now = sums(residual, precond, image)
            ratio_next = gamma_next / gamma_now
            step_size = gamma_next / (delta_now - ratio_next * gamma_next / step_size)
            direction = precond + ratio_next * direction
            along_dir = image + ratio_next * along_dir
            gamma_now = gamma_next
    return (surface, residual)


def solution(mesh):
    torus = Mesh(mesh.devices.reshape(8, 8, 4, 2, 2), ("lon_0", "lon_1", "lon_2", "lat_0", "lat_1"))
    in_specs = (
        P(None, LON, LAT),
        P(None, LON, LAT),
        P(),
        P(LON, LAT),
        P(LON, LAT),
        P(LON, LAT),
        P(LON, LAT),
    )
    out_specs = (P(LON, LAT), P(LON, LAT))
    return jax.shard_map(body, mesh=torus, in_specs=in_specs, out_specs=out_specs, check_vma=False)
```

profile of v0, /device:TPU:1, one launch (start us, length us, event | category | flops | bytes accessed | tf_op | source)
XLA Modules:
  0.0 275.8 jit_solution(13259526267617752389)
XLA Ops:
  0.7 1.1 copy-done
  1.7 1.4 fusion.2
  3.2 0.8 fusion
  6.9 3.9 %collective-permute-start = (f32[6,2,512]{2,1,0:T(2,128)S(1)}, f32[6,2,512]{2,1,0:T(2,128)S(1)}, u32[]{:S(2)}, u32[]{:S(2)}) collective-permute-start(f32[6,2,512]{2,1,0:T(2,128)S(1)} %get-tuple-element.57), channel_id=1, source_target_pairs={{0,4},{4,8},{8,12},{12,16},{16,20},{20,24},{24,28},{28,32},{32,36}... | collective-permute-start | bytes 73736 | tf_op jit(solution)/shard_map/ppermute | solution.py:43
  10.8 22.3 %collective-permute-start.1 = (f32[6,2,512]{2,1,0:T(2,128)S(1)}, f32[6,2,512]{2,1,0:T(2,128)S(1)}, u32[]{:S(2)}, u32[]{:S(2)}) collective-permute-start(f32[6,2,512]{2,1,0:T(2,128)S(1)} %get-tuple-element.58), channel_id=1, source_target_pairs={{4,0},{8,4},{12,8},{16,12},{20,16},{24,20},{28,24},{32,28},{36,32}... | collective-permute-start | bytes 73736 | tf_op jit(solution)/shard_map/ppermute | solution.py:46
  33.2 0.9 collective-permute-done.1
  34.2 5.8 %collective-permute-start.2 = (f32[6,12,2]{2,1,0:T(8,128)S(1)}, f32[6,12,2]{2,1,0:T(8,128)S(1)}, u32[]{:S(2)}, u32[]{:S(2)}) collective-permute-start(f32[6,12,2]{2,1,0:T(8,128)S(1)} %get-tuple-element.55), channel_id=1, source_target_pairs={{0,1},{1,2},{2,3},{3,0},{4,5},{5,6},{6,7},{7,4},{8,9},{9,10},{10,1... | collective-permute-start | bytes 1736 | tf_op jit(solution)/shard_map/ppermute | solution.py:43
  40.0 1.9 collective-permute-start.3
  42.0 7.4 %collective-permute-done.3 = f32[6,12,2]{2,1,0:T(8,128)S(1)} collective-permute-done((f32[6,12,2]{2,1,0:T(8,128)S(1)}, f32[6,12,2]{2,1,0:T(8,128)S(1)}, u32[]{:S(2)}, u32[]{:S(2)}) %collective-permute-start.3) | collective-permute-done | bytes 608 | tf_op jit(solution)/shard_map/ppermute | solution.py:46
  50.6 14.2 %all-reduce.9 = (f32[]{:T(128)}, f32[]{:T(128)}) all-reduce(f32[]{:T(128)} %get-tuple-element.3, f32[]{:T(128)} %get-tuple-element.2), channel_id=1, replica_groups=mesh['lon_0'=8,'lon_1'=8,'lon_2'=4,'lat_0'=2,'lat_1'=2] {'lon_0'}, use_global_device_ids=true, to_apply=%region_1.2 | all-reduce | flops 2 | bytes 16 | tf_op jit(solution)/shard_map/psum | solution.py:52
  64.8 13.3 %all-reduce.6 = (f32[]{:T(128)}, f32[]{:T(128)}) all-reduce(f32[]{:T(128)} %get-tuple-element.18, f32[]{:T(128)} %get-tuple-element.19), channel_id=1, replica_groups=mesh['lon_0'=8,'lon_1'=8,'lon_2'=4,'lat_0'=2,'lat_1'=2] {'lon_1'}, use_global_device_ids=true, to_apply=%region_2.3 | all-reduce | flops 2 | bytes 16 | tf_op jit(solution)/shard_map/psum | solution.py:52
  78.1 12.2 %all-reduce.12 = (f32[]{:T(128)}, f32[]{:T(128)}) all-reduce(f32[]{:T(128)} %get-tuple-element.12, f32[]{:T(128)} %get-tuple-element.13), channel_id=1, replica_groups=mesh['lon_0'=8,'lon_1'=8,'lon_2'=4,'lat_0'=2,'lat_1'=2] {'lon_2'}, use_global_device_ids=true, to_apply=%region_3.4 | all-reduce | flops 2 | bytes 16 | tf_op jit(solution)/shard_map/psum | solution.py:52
  90.3 8.3 %all-reduce.18 = (f32[]{:T(128)}, f32[]{:T(128)}) all-reduce(f32[]{:T(128)} %get-tuple-element.24, f32[]{:T(128)} %get-tuple-element.25), channel_id=1, replica_groups=mesh['lon_0'=8,'lon_1'=8,'lon_2'=4,'lat_0'=2,'lat_1'=2] {'lat_0'}, use_global_device_ids=true, to_apply=%region_4.5 | all-reduce | flops 2 | bytes 16 | tf_op jit(solution)/shard_map/psum | solution.py:52
  98.6 9.7 %all-reduce.15 = (f32[]{:T(128)}, f32[]{:T(128)}) all-reduce(f32[]{:T(128)} %get-tuple-element.36, f32[]{:T(128)} %get-tuple-element.37), channel_id=1, replica_groups=mesh['lon_0'=8,'lon_1'=8,'lon_2'=4,'lat_0'=2,'lat_1'=2] {'lat_1'}, use_global_device_ids=true, to_apply=%region_5.6 | all-reduce | flops 2 | bytes 16 | tf_op jit(solution)/shard_map/psum | solution.py:52
  109.8 1.9 collective-permute-start.5
  111.7 9.4 %collective-permute-start.4 = (f32[1,512]{1,0:T(1,128)S(1)}, f32[1,512]{1,0:T(1,128)S(1)}, u32[]{:S(2)}, u32[]{:S(2)}) collective-permute-start(f32[1,512]{1,0:T(1,128)S(1)} %get-tuple-element.68), channel_id=1, source_target_pairs={{4,0},{8,4},{12,8},{16,12},{20,16},{24,20},{28,24},{32,28},{36,32}... | collective-permute-start | bytes 6152 | tf_op jit(solution)/shard_map/ppermute | solution.py:26
  121.1 2.8 %collective-permute-start.6 = (f32[8,1]{1,0:T(8,128)S(1)}, f32[8,1]{1,0:T(8,128)S(1)}, u32[]{:S(2)}, u32[]{:S(2)}) collective-permute-start(f32[8,1]{1,0:T(8,128)S(1)} %get-tuple-element.65), channel_id=1, source_target_pairs={{1,0},{2,1},{3,2},{0,3},{5,4},{6,5},{7,6},{4,7},{9,8},{10,9},{11,1... | collective-permute-start | bytes 104 | tf_op jit(solution)/shard_map/ppermute | solution.py:26
  124.0 6.7 %collective-permute-start.7 = (f32[8,1]{1,0:T(8,128)S(1)}, f32[8,1]{1,0:T(8,128)S(1)}, u32[]{:S(2)}, u32[]{:S(2)}) collective-permute-start(f32[8,1]{1,0:T(8,128)S(1)} %get-tuple-element.66), channel_id=1, source_target_pairs={{0,1},{1,2},{2,3},{3,0},{4,5},{5,6},{6,7},{7,4},{8,9},{9,10},{10,1... | collective-permute-start | bytes 104 | tf_op jit(solution)/shard_map/ppermute | solution.py:25
  132.1 11.6 %all-reduce.8 = (f32[]{:T(128)}, f32[]{:T(128)}) all-reduce(f32[]{:T(128)} %get-tuple-element.7, f32[]{:T(128)} %get-tuple-element.6), channel_id=1, replica_groups=mesh['lon_0'=8,'lon_1'=8,'lon_2'=4,'lat_0'=2,'lat_1'=2] {'lon_0'}, use_global_device_ids=true, to_apply=%region_13.14 | all-reduce | flops 2 | bytes 16 | tf_op jit(solution)/shard_map/psum | solution.py:52
  143.7 11.4 %all-reduce.5 = (f32[]{:T(128)}, f32[]{:T(128)}) all-reduce(f32[]{:T(128)} %get-tuple-element.16, f32[]{:T(128)} %get-tuple-element.17), channel_id=1, replica_groups=mesh['lon_0'=8,'lon_1'=8,'lon_2'=4,'lat_0'=2,'lat_1'=2] {'lon_1'}, use_global_device_ids=true, to_apply=%region_14.15 | all-reduce | flops 2 | bytes 16 | tf_op jit(solution)/shard_map/psum | solution.py:52
  155.1 8.0 %all-reduce.11 = (f32[]{:T(128)}, f32[]{:T(128)}) all-reduce(f32[]{:T(128)} %get-tuple-element.10, f32[]{:T(128)} %get-tuple-element.11), channel_id=1, replica_groups=mesh['lon_0'=8,'lon_1'=8,'lon_2'=4,'lat_0'=2,'lat_1'=2] {'lon_2'}, use_global_device_ids=true, to_apply=%region_15.16 | all-reduce | flops 2 | bytes 16 | tf_op jit(solution)/shard_map/psum | solution.py:52
  163.1 8.4 %all-reduce.17 = (f32[]{:T(128)}, f32[]{:T(128)}) all-reduce(f32[]{:T(128)} %get-tuple-element.22, f32[]{:T(128)} %get-tuple-element.23), channel_id=1, replica_groups=mesh['lon_0'=8,'lon_1'=8,'lon_2'=4,'lat_0'=2,'lat_1'=2] {'lat_0'}, use_global_device_ids=true, to_apply=%region_16.17 | all-reduce | flops 2 | bytes 16 | tf_op jit(solution)/shard_map/psum | solution.py:52
  171.4 17.6 %all-reduce.14 = (f32[]{:T(128)}, f32[]{:T(128)}) all-reduce(f32[]{:T(128)} %get-tuple-element.34, f32[]{:T(128)} %get-tuple-element.35), channel_id=1, replica_groups=mesh['lon_0'=8,'lon_1'=8,'lon_2'=4,'lat_0'=2,'lat_1'=2] {'lat_1'}, use_global_device_ids=true, to_apply=%region_17.18 | all-reduce | flops 2 | bytes 16 | tf_op jit(solution)/shard_map/psum | solution.py:52
  193.8 2.2 collective-permute-start.9
  196.0 9.1 %collective-permute-start.8 = (f32[1,512]{1,0:T(1,128)S(1)}, f32[1,512]{1,0:T(1,128)S(1)}, u32[]{:S(2)}, u32[]{:S(2)}) collective-permute-start(f32[1,512]{1,0:T(1,128)S(1)} %get-tuple-element.64), channel_id=1, source_target_pairs={{4,0},{8,4},{12,8},{16,12},{20,16},{24,20},{28,24},{32,28},{36,32}... | collective-permute-start | bytes 6152 | tf_op jit(solution)/shard_map/ppermute | solution.py:26
  205.2 2.8 %collective-permute-start.10 = (f32[8,1]{1,0:T(8,128)S(1)}, f32[8,1]{1,0:T(8,128)S(1)}, u32[]{:S(2)}, u32[]{:S(2)}) collective-permute-start(f32[8,1]{1,0:T(8,128)S(1)} %get-tuple-element.61), channel_id=1, source_target_pairs={{1,0},{2,1},{3,2},{0,3},{5,4},{6,5},{7,6},{4,7},{9,8},{10,9},{11,1... | collective-permute-start | bytes 104 | tf_op jit(solution)/shard_map/ppermute | solution.py:26
  208.0 6.7 %collective-permute-start.11 = (f32[8,1]{1,0:T(8,128)S(1)}, f32[8,1]{1,0:T(8,128)S(1)}, u32[]{:S(2)}, u32[]{:S(2)}) collective-permute-start(f32[8,1]{1,0:T(8,128)S(1)} %get-tuple-element.62), channel_id=1, source_target_pairs={{0,1},{1,2},{2,3},{3,0},{4,5},{5,6},{6,7},{7,4},{8,9},{9,10},{10,1... | collective-permute-start | bytes 104 | tf_op jit(solution)/shard_map/ppermute | solution.py:25
  216.1 11.3 %all-reduce.7 = (f32[]{:T(128)}, f32[]{:T(128)}) all-reduce(f32[]{:T(128)} %get-tuple-element.5, f32[]{:T(128)} %get-tuple-element.4), channel_id=1, replica_groups=mesh['lon_0'=8,'lon_1'=8,'lon_2'=4,'lat_0'=2,'lat_1'=2] {'lon_0'}, use_global_device_ids=true, to_apply=%region_25.26 | all-reduce | flops 2 | bytes 16 | tf_op jit(solution)/shard_map/psum | solution.py:52
  227.4 11.3 %all-reduce.4 = (f32[]{:T(128)}, f32[]{:T(128)}) all-reduce(f32[]{:T(128)} %get-tuple-element.14, f32[]{:T(128)} %get-tuple-element.15), channel_id=1, replica_groups=mesh['lon_0'=8,'lon_1'=8,'lon_2'=4,'lat_0'=2,'lat_1'=2] {'lon_1'}, use_global_device_ids=true, to_apply=%region_26.27 | all-reduce | flops 2 | bytes 16 | tf_op jit(solution)/shard_map/psum | solution.py:52
  238.7 8.3 %all-reduce.10 = (f32[]{:T(128)}, f32[]{:T(128)}) all-reduce(f32[]{:T(128)} %get-tuple-element.8, f32[]{:T(128)} %get-tuple-element.9), channel_id=1, replica_groups=mesh['lon_0'=8,'lon_1'=8,'lon_2'=4,'lat_0'=2,'lat_1'=2] {'lon_2'}, use_global_device_ids=true, to_apply=%region_27.28 | all-reduce | flops 2 | bytes 16 | tf_op jit(solution)/shard_map/psum | solution.py:52
  247.0 8.3 %all-reduce.16 = (f32[]{:T(128)}, f32[]{:T(128)}) all-reduce(f32[]{:T(128)} %get-tuple-element.20, f32[]{:T(128)} %get-tuple-element.21), channel_id=1, replica_groups=mesh['lon_0'=8,'lon_1'=8,'lon_2'=4,'lat_0'=2,'lat_1'=2] {'lat_0'}, use_global_device_ids=true, to_apply=%region_28.29 | all-reduce | flops 2 | bytes 16 | tf_op jit(solution)/shard_map/psum | solution.py:52
  255.3 15.7 %all-reduce.13 = (f32[]{:T(128)}, f32[]{:T(128)}) all-reduce(f32[]{:T(128)} %get-tuple-element.32, f32[]{:T(128)} %get-tuple-element.33), channel_id=1, replica_groups=mesh['lon_0'=8,'lon_1'=8,'lon_2'=4,'lat_0'=2,'lat_1'=2] {'lat_1'}, use_global_device_ids=true, to_apply=%region_29.30 | all-reduce | flops 2 | bytes 16 | tf_op jit(solution)/shard_map/psum | solution.py:52
  (47 shorter events, 8.2 us)
Async XLA Ops:
  0.6 1.1 copy-start
  0.6 2.5 copy-start.6
  0.7 2.5 copy-start.1
  4.0 0.7 copy-start.2
  4.7 0.7 copy-start.3
  5.4 0.7 copy-start.4
  6.1 0.7 copy-start.5
  6.9 26.3 %collective-permute-start = (f32[6,2,512]{2,1,0:T(2,128)S(1)}, f32[6,2,512]{2,1,0:T(2,128)S(1)}, u32[]{:S(2)}, u32[]{:S(2)}) collective-permute-start(f32[6,2,512]{2,1,0:T(2,128)S(1)} %get-tuple-element.57), channel_id=1, source_target_pairs={{0,4},{4,8},{8,12},{12,16},{16,20},{20,24},{24,28},{28,32},{32,36}... | collective-permute-start | bytes 73736 | tf_op jit(solution)/shard_map/ppermute | solution.py:43
  10.8 23.3 %collective-permute-start.1 = (f32[6,2,512]{2,1,0:T(2,128)S(1)}, f32[6,2,512]{2,1,0:T(2,128)S(1)}, u32[]{:S(2)}, u32[]{:S(2)}) collective-permute-start(f32[6,2,512]{2,1,0:T(2,128)S(1)} %get-tuple-element.58), channel_id=1, source_target_pairs={{4,0},{8,4},{12,8},{16,12},{20,16},{24,20},{28,24},{32,28},{36,32}... | collective-permute-start | bytes 73736 | tf_op jit(solution)/shard_map/ppermute | solution.py:46
  34.2 7.8 %collective-permute-start.2 = (f32[6,12,2]{2,1,0:T(8,128)S(1)}, f32[6,12,2]{2,1,0:T(8,128)S(1)}, u32[]{:S(2)}, u32[]{:S(2)}) collective-permute-start(f32[6,12,2]{2,1,0:T(8,128)S(1)} %get-tuple-element.55), channel_id=1, source_target_pairs={{0,1},{1,2},{2,3},{3,0},{4,5},{5,6},{6,7},{7,4},{8,9},{9,10},{10,1... | collective-permute-start | bytes 1736 | tf_op jit(solution)/shard_map/ppermute | solution.py:43
  40.0 9.3 %collective-permute-start.3 = (f32[6,12,2]{2,1,0:T(8,128)S(1)}, f32[6,12,2]{2,1,0:T(8,128)S(1)}, u32[]{:S(2)}, u32[]{:S(2)}) collective-permute-start(f32[6,12,2]{2,1,0:T(8,128)S(1)} %get-tuple-element.56), channel_id=1, source_target_pairs={{1,0},{2,1},{3,2},{0,3},{5,4},{6,5},{7,6},{4,7},{9,8},{10,9},{11,1... | collective-permute-start | bytes 1736 | tf_op jit(solution)/shard_map/ppermute | solution.py:46
  109.8 21.6 %collective-permute-start.5 = (f32[1,512]{1,0:T(1,128)S(1)}, f32[1,512]{1,0:T(1,128)S(1)}, u32[]{:S(2)}, u32[]{:S(2)}) collective-permute-start(f32[1,512]{1,0:T(1,128)S(1)} %get-tuple-element.67), channel_id=1, source_target_pairs={{0,4},{4,8},{8,12},{12,16},{16,20},{20,24},{24,28},{28,32},{32,36}... | collective-permute-start | bytes 6152 | tf_op jit(solution)/shard_map/ppermute | solution.py:25
  111.7 19.7 %collective-permute-start.4 = (f32[1,512]{1,0:T(1,128)S(1)}, f32[1,512]{1,0:T(1,128)S(1)}, u32[]{:S(2)}, u32[]{:S(2)}) collective-permute-start(f32[1,512]{1,0:T(1,128)S(1)} %get-tuple-element.68), channel_id=1, source_target_pairs={{4,0},{8,4},{12,8},{16,12},{20,16},{24,20},{28,24},{32,28},{36,32}... | collective-permute-start | bytes 6152 | tf_op jit(solution)/shard_map/ppermute | solution.py:26
  121.1 9.5 %collective-permute-start.6 = (f32[8,1]{1,0:T(8,128)S(1)}, f32[8,1]{1,0:T(8,128)S(1)}, u32[]{:S(2)}, u32[]{:S(2)}) collective-permute-start(f32[8,1]{1,0:T(8,128)S(1)} %get-tuple-element.65), channel_id=1, source_target_pairs={{1,0},{2,1},{3,2},{0,3},{5,4},{6,5},{7,6},{4,7},{9,8},{10,9},{11,1... | collective-permute-start | bytes 104 | tf_op jit(solution)/shard_map/ppermute | solution.py:26
  124.0 7.4 %collective-permute-start.7 = (f32[8,1]{1,0:T(8,128)S(1)}, f32[8,1]{1,0:T(8,128)S(1)}, u32[]{:S(2)}, u32[]{:S(2)}) collective-permute-start(f32[8,1]{1,0:T(8,128)S(1)} %get-tuple-element.66), channel_id=1, source_target_pairs={{0,1},{1,2},{2,3},{3,0},{4,5},{5,6},{6,7},{7,4},{8,9},{9,10},{10,1... | collective-permute-start | bytes 104 | tf_op jit(solution)/shard_map/ppermute | solution.py:25
  193.8 21.6 %collective-permute-start.9 = (f32[1,512]{1,0:T(1,128)S(1)}, f32[1,512]{1,0:T(1,128)S(1)}, u32[]{:S(2)}, u32[]{:S(2)}) collective-permute-start(f32[1,512]{1,0:T(1,128)S(1)} %get-tuple-element.63), channel_id=1, source_target_pairs={{0,4},{4,8},{8,12},{12,16},{16,20},{20,24},{24,28},{28,32},{32,36}... | collective-permute-start | bytes 6152 | tf_op jit(solution)/shard_map/ppermute | solution.py:25
  196.0 19.4 %collective-permute-start.8 = (f32[1,512]{1,0:T(1,128)S(1)}, f32[1,512]{1,0:T(1,128)S(1)}, u32[]{:S(2)}, u32[]{:S(2)}) collective-permute-start(f32[1,512]{1,0:T(1,128)S(1)} %get-tuple-element.64), channel_id=1, source_target_pairs={{4,0},{8,4},{12,8},{16,12},{20,16},{24,20},{28,24},{32,28},{36,32}... | collective-permute-start | bytes 6152 | tf_op jit(solution)/shard_map/ppermute | solution.py:26
  205.2 9.5 %collective-permute-start.10 = (f32[8,1]{1,0:T(8,128)S(1)}, f32[8,1]{1,0:T(8,128)S(1)}, u32[]{:S(2)}, u32[]{:S(2)}) collective-permute-start(f32[8,1]{1,0:T(8,128)S(1)} %get-tuple-element.61), channel_id=1, source_target_pairs={{1,0},{2,1},{3,2},{0,3},{5,4},{6,5},{7,6},{4,7},{9,8},{10,9},{11,1... | collective-permute-start | bytes 104 | tf_op jit(solution)/shard_map/ppermute | solution.py:26
  208.0 7.4 %collective-permute-start.11 = (f32[8,1]{1,0:T(8,128)S(1)}, f32[8,1]{1,0:T(8,128)S(1)}, u32[]{:S(2)}, u32[]{:S(2)}) collective-permute-start(f32[8,1]{1,0:T(8,128)S(1)} %get-tuple-element.62), channel_id=1, source_target_pairs={{0,1},{1,2},{2,3},{3,0},{4,5},{5,6},{6,7},{7,4},{8,9},{9,10},{10,1... | collective-permute-start | bytes 104 | tf_op jit(solution)/shard_map/ppermute | solution.py:25
where the time goes:
time: 277 us; the launch traced here: 276 us
  blocking collectives  170 us (61%)
  starting transfers between devices  75.5 us (27%)
  between operations  11 us (4%)
  waiting for transfers between devices  9.73 us (4%)
  local copies, waits for them, and re-layouts  4.11 us (1%)
  other arithmetic  3.66 us (1%)
    psum x15, blocking collectives, by_axis(): return functools.reduce(lax.psum, axes, value)  170 us
    ppermute x2, starting transfers between devices, extended_2(): lax.ppermute(lax.slice_in_dim(block, 0, width, axis=dim), axis, backward)  24.2 us
    ppermute x4, starting transfers between devices, padded_2(): lax.ppermute(leading, axis, [(b, a) for a, b in up])  24.1 us
    ppermute x4, starting transfers between devices, padded_2(): lax.ppermute(last, axis, up)  17.4 us
    ppermute x2, starting transfers between devices, extended_2(): lax.ppermute(lax.slice_in_dim(block, block.shape[dim] - width, None, axis...  9.77 us
    ppermute x2, waiting for transfers between devices, extended_2(): lax.ppermute(lax.slice_in_dim(block, 0, width, axis=dim), axis, backward)  8.27 us
  transfers between devices with their start and end apart: 12, of which 4 were waited for; matrix products, arithmetic and copies ran while one was open for 0% of the time, Pallas kernels for 0%

commit v1 on v0

v1 whole, which is shorter than its diff:
```python
import functools
import math

import jax
import jax.numpy as jnp
from jax import lax
from jax.experimental import pallas as pl
from jax.experimental.pallas import tpu as pltpu
from jax.sharding import Mesh
from jax.sharding import PartitionSpec as P

LEVELS = 40
CHUNKS = 4
ROWS = 8
COLS = 512
FIELDS = 6
LON = ("lon_0", "lon_1", "lon_2")
LAT = ("lat_0", "lat_1")
NEAR = ("lon_2", "lat_0", "lat_1")
FAR = ("lon_0", "lon_1")
SCALE = 1.0 / math.sqrt(LEVELS)
VMEM = pl.BlockSpec(memory_space=pltpu.VMEM)
ANY = pl.BlockSpec(memory_space=pl.ANY)
SMEM = pl.BlockSpec(memory_space=pltpu.SMEM)


def lon_even():
    return lax.rem(lax.axis_index("lon_2"), 2) == 0


def lat_even():
    return lax.axis_index("lat_1") == 0


def pick(flag, yes, no):
    return jnp.where(jnp.full(yes.shape, flag), yes, no)


def sublane(shape):
    return lax.broadcasted_iota(jnp.int32, shape, len(shape) - 2)


def lane(shape):
    return lax.broadcasted_iota(jnp.int32, shape, len(shape) - 1)


def sum_kernel(thick, u, v, depth, mask, damping, eta, own, odd, even, u_buf, v_buf, f_buf, m_buf, sems, f_sems):
    step = LEVELS // CHUNKS
    copies = []
    for c in range(CHUNKS):
        part = pl.ds(c * step, step)
        copies.append(
            (
                pltpu.make_async_copy(u.at[part], u_buf.at[part], sems.at[0, c]),
                pltpu.make_async_copy(v.at[part], v_buf.at[part], sems.at[1, c]),
            )
        )
    small = [
        pltpu.make_async_copy(depth, f_buf.at[0], f_sems.at[0]),
        pltpu.make_async_copy(damping, f_buf.at[1], f_sems.at[1]),
        pltpu.make_async_copy(eta, f_buf.at[2], f_sems.at[2]),
        pltpu.make_async_copy(mask, m_buf, f_sems.at[3]),
    ]
    for a, b in copies:
        a.start()
        b.start()
    for s in small:
        s.start()
    total = [jnp.zeros((ROWS, COLS), jnp.float32), jnp.zeros((ROWS, COLS), jnp.float32)]
    for c in range(CHUNKS):
        for i, buf in enumerate((u_buf, v_buf)):
            copies[c][i].wait()
            for k in range(c * step, (c + 1) * step):
                total[i] = total[i] + thick[k] * buf[k]
    for s in small:
        s.wait()
    wet = m_buf[...].astype(jnp.float32)
    fields = [total[0] * SCALE, total[1] * SCALE, f_buf[0], wet, f_buf[1], f_buf[2]]
    for i, field in enumerate(fields):
        own[i] = field
    high = sublane((ROWS, COLS)) >= ROWS // 2
    flag = lon_even()
    for p in range(FIELDS // 2):
        a, b = fields[2 * p], pltpu.roll(fields[2 * p + 1], ROWS // 2, 0)
        first = jnp.where(high, b, a)
        last = jnp.where(high, a, b)
        even[p] = pick(flag, last, first)
        odd[p] = pick(flag, first, last)


def join_kernel(own, got_odd, got_even, halo, mid, core):
    flag = lon_even()
    side = lat_even()
    high = sublane((ROWS, COLS)) >= ROWS // 2
    rows = []
    for p in range(FIELDS // 2):
        above = pick(flag, got_even[p], got_odd[p])
        below = pick(flag, got_odd[p], got_even[p])
        rows.append(jnp.where(high, below, above))
        rows.append(pltpu.roll(jnp.where(high, above, below), ROWS // 2, 0))
    for i in range(FIELDS):
        halo[i] = rows[i]
        for t, tile in enumerate((own[i], rows[i])):
            first = tile[:, :128]
            last = tile[:, COLS - 128 :]
            core[2 * i + t] = pick(side, last, first)
            mid[2 * i + t] = pick(side, first, last)


def basis_kernel(own, halo, got_mid, got_core, basis, moments):
    side = lat_even()
    right = lane((ROWS, 128)) >= 64
    fields = []
    for i in range(FIELDS):
        tiles = []
        for t, tile in enumerate((own[i], halo[i])):
            above = pick(side, got_core[2 * i + t], got_mid[2 * i + t])
            below = pick(side, got_mid[2 * i + t], got_core[2 * i + t])
            tiles.append(jnp.concatenate([tile, jnp.where(right, below, above)], axis=1))
        fields.append(jnp.concatenate(tiles, axis=0))
    sum_east, sum_north, depth, wet, damping, eta = fields
    rows, cols = 2 * ROWS, COLS + 128

    def east(a):
        return pltpu.roll(a, rows - 1, 0)

    def west(a):
        return pltpu.roll(a, 1, 0)

    def north(a):
        return pltpu.roll(a, cols - 1, 1)

    def south(a):
        return pltpu.roll(a, 1, 1)

    wet_x = wet * east(wet)
    wet_y = wet * north(wet)
    face_x = wet_x * 0.5 * (depth + east(depth))
    face_y = wet_y * 0.5 * (depth + north(depth))
    flux_x = wet_x * sum_east
    flux_y = wet_y * sum_north
    diverge = flux_x - west(flux_x) + flux_y - south(flux_y)
    rhs = wet * (damping * eta - diverge)
    back_x, back_y = west(face_x), south(face_y)
    diag = damping + face_x + back_x + face_y + back_y
    diag = jnp.where(diag > 0.0, diag, 1.0)

    def spread(a):
        return face_x * east(a) + back_x * west(a) + face_y * north(a) + back_y * south(a)

    def mine(a):
        return a[:ROWS, :COLS]

    w0 = rhs
    v0 = w0 / diag
    w1 = spread(v0)
    v1 = w1 / diag
    w2 = spread(v1)
    v2 = w2 / diag
    w3 = spread(v2)
    parts = [mine(a) for a in (v0, v1, v2, w0, w1, w2, w3)]
    for i, part in enumerate(parts):
        basis[i] = part
    v0, v1, v2, w0, w1, w2, w3 = parts
    row = jnp.zeros((1, 128), jnp.float32)
    spot = lane((1, 128))
    for k, (a, b) in enumerate(((v0, w0), (v0, w1), (v1, w1), (v1, w2), (v2, w2), (v2, w3))):
        prod = a * b
        prod = prod[:, :128] + prod[:, 128:256] + (prod[:, 256:384] + prod[:, 384:])
        total = jnp.sum(jnp.sum(prod, axis=0, keepdims=True), axis=1, keepdims=True)
        row = jnp.where(spot == k, total, row)
    moments[...] = jnp.broadcast_to(row, moments.shape)


def relay_kernel(parts, out):
    out[...] = jnp.broadcast_to(jnp.sum(parts[...], axis=0, keepdims=True), out.shape)


def poly(a, b, scale):
    size = max(len(a), len(b))
    out = []
    for i in range(size):
        if i >= len(b):
            out.append(a[i])
        elif i >= len(a):
            out.append(scale * b[i])
        else:
            out.append(a[i] + scale * b[i])
    return out


def dot(a, b, moments, shift=0):
    total = None
    for k in range(len(a) + len(b) - 1):
        coef = None
        for i in range(len(a)):
            j = k - i
            if 0 <= j < len(b):
                term = a[i] * b[j]
                coef = term if coef is None else coef + term
        term = coef * moments[k + shift]
        total = term if total is None else total + term
    return total


def final_kernel(parts, basis, surface, residual):
    row = jnp.sum(parts[...], axis=0, keepdims=True)
    spot = lane((1, 128))
    moments = [jnp.sum(jnp.where(spot == k, row, 0.0), axis=1, keepdims=True) for k in range(6)]
    one = jnp.ones((1, 1), jnp.float32)
    gaps = [moments[k] - moments[k + 1] for k in range(5)]
    pre = [one]
    gamma = moments[0]
    step = gamma / gaps[0]
    direction = pre
    answer = [step]
    for sweep in range(3):
        image = [direction[0]]
        for i in range(1, len(direction)):
            image.append(direction[i] - direction[i - 1])
        image.append(-direction[-1])
        pre = poly(pre, image, -step)
        if sweep == 2:
            break
        gamma_next = dot(pre, pre, moments)
        delta = dot(pre, pre, gaps)
        ratio = gamma_next / gamma
        step = gamma_next / (delta - ratio * gamma_next / step)
        direction = poly(pre, direction, ratio)
        answer = poly(answer, direction, step)
        gamma = gamma_next
    surface[...] = answer[0] * basis[0] + answer[1] * basis[1] + answer[2] * basis[2]
    residual[...] = (pre[0] * basis[3] + pre[1] * basis[4]) + (pre[2] * basis[5] + pre[3] * basis[6])


def shape(*dims):
    return jax.ShapeDtypeStruct(dims, jnp.float32)


def total_over(rows, axes):
    return lax.all_to_all(rows, axes, 0, 0, tiled=True)


def body(u_vel, v_vel, thickness, depth, sea_mask, damping, eta_prev):
    count = lax.axis_size(LON)
    pairs_even = [(i, i ^ 1) for i in range(count)]
    pairs_odd = [(i, (i + 1) % count) if i % 2 else (i, (i - 1) % count) for i in range(count)]
    pairs_core = [(0, 1), (1, 0), (2, 3), (3, 2)]
    pairs_mid = [(1, 2), (2, 1)]
    own, odd, even = pl.pallas_call(
        sum_kernel,
        out_shape=(shape(FIELDS, ROWS, COLS), shape(3, ROWS, COLS), shape(3, ROWS, COLS)),
        in_specs=[SMEM] + [ANY] * 6,
        out_specs=(VMEM, VMEM, VMEM),
        scratch_shapes=[
            pltpu.VMEM((LEVELS, ROWS, COLS), jnp.float32),
            pltpu.VMEM((LEVELS, ROWS, COLS), jnp.float32),
            pltpu.VMEM((3, ROWS, COLS), jnp.float32),
            pltpu.VMEM((ROWS, COLS), jnp.int32),
            pltpu.SemaphoreType.DMA((2, CHUNKS)),
            pltpu.SemaphoreType.DMA((4,)),
        ],
        name="sums",
    )(thickness, u_vel, v_vel, depth, sea_mask, damping, eta_prev)
    got_odd = lax.ppermute(odd, LON, pairs_odd)
    got_even = lax.ppermute(even, LON, pairs_even)
    halo, mid, core = pl.pallas_call(
        join_kernel,
        out_shape=(shape(FIELDS, ROWS, COLS), shape(12, ROWS, 128), shape(12, ROWS, 128)),
        in_specs=[VMEM] * 3,
        out_specs=(VMEM,) * 3,
        name="join",
    )(own, got_odd, got_even)
    got_mid = lax.ppermute(mid, LAT, pairs_mid)
    got_core = lax.ppermute(core, LAT, pairs_core)
    near = lax.axis_size(NEAR)
    far = lax.axis_size(FAR)
    basis, moments = pl.pallas_call(
        basis_kernel,
        out_shape=(shape(7, ROWS, COLS), shape(near, 128)),
        in_specs=[VMEM] * 4,
        out_specs=(VMEM,) * 2,
        name="basis",
    )(own, halo, got_mid, got_core)
    moments = total_over(moments, NEAR)
    moments = pl.pallas_call(
        relay_kernel, out_shape=shape(far, 128), in_specs=[VMEM], out_specs=VMEM, name="relay"
    )(moments)
    moments = total_over(moments, FAR)
    return pl.pallas_call(
        final_kernel,
        out_shape=(shape(ROWS, COLS), shape(ROWS, COLS)),
        in_specs=[VMEM] * 2,
        out_specs=(VMEM,) * 2,
        name="final",
    )(moments, basis)


def solution(mesh):
    torus = Mesh(mesh.devices.reshape(8, 8, 4, 2, 2), LON + LAT)
    wide = P(None, LON, LAT)
    flat = P(LON, LAT)
    return jax.shard_map(
        body,
        mesh=torus,
        in_specs=(wide, wide, P(), flat, flat, flat, flat),
        out_specs=(flat, flat),
        check_vma=False,
    )
```

time: 277 us -> 80.8 us (0.29)
  blocking collectives: 170 us -> 29.9 us
  starting transfers between devices: 75.5 us -> 34.6 us
  between operations: 11 us -> 0.7 us
  Pallas kernels: 0 us -> 9.53 us
  waiting for transfers between devices: 9.73 us -> 4.5 us
  other arithmetic: 3.66 us -> 0 us
  local copies, waits for them, and re-layouts: 4.11 us -> 1.23 us
    psum x15 -> x0, blocking collectives: 170 us -> none  [by_axis(): return functools.reduce(lax.psum, axes, value)]
    ppermute x12 -> x4, starting transfers between devices: 75.5 us -> 34.6 us  [the longest x1 24.3 us: body(): got_odd = lax.ppermute(odd, LON, pairs_odd)]
    all_to_all x0 -> x2, blocking collectives: none -> 29.9 us  [total_over(): return lax.all_to_all(rows, axes, 0, 0, tiled=True)]
    pallas_call x0 -> x5, Pallas kernels: none -> 9.53 us  [the longest x1 2.9 us: body(): pl.pallas_call(sum_kernel, out_shape=(shape(FIELDS, ROWS, COLS), shape(3,...]
    ppermute x12 -> x4, waiting for transfers between devices: 9.73 us -> 4.5 us  [the longest x1 3.1 us: body(): got_even = lax.ppermute(even, LON, pairs_even)]
  transfers between devices with their start and end apart: 12 -> 4, of which waited for: 4 -> 3; matrix products, arithmetic and copies ran while one was open for 0% -> 0% of each run, Pallas kernels for 0% -> 0%
where the time goes in v1:
time: 80.8 us; the launch traced here: 80.4 us
  starting transfers between devices  34.6 us (43%)
  blocking collectives  29.9 us (37%)
  Pallas kernels  9.53 us (12%)
  waiting for transfers between devices  4.5 us (6%)
  local copies, waits for them, and re-layouts  1.23 us (2%)
    all_to_all x2, blocking collectives, total_over(): return lax.all_to_all(rows, axes, 0, 0, tiled=True)  29.9 us
    ppermute x1, starting transfers between devices, body(): got_odd = lax.ppermute(odd, LON, pairs_odd)  24.3 us
    ppermute x1, starting transfers between devices, body(): got_mid = lax.ppermute(mid, LAT, pairs_mid)  6.39 us
    ppermute x1, waiting for transfers between devices, body(): got_even = lax.ppermute(even, LON, pairs_even)  3.1 us
    pallas_call x1, Pallas kernels, body(): pl.pallas_call(sum_kernel, out_shape=(shape(FIELDS, ROWS, COLS), shape(3,...  2.9 us
    pallas_call x1, Pallas kernels, body(): pl.pallas_call(basis_kernel, out_shape=(shape(7, ROWS, COLS), shape(near,...  2.02 us
    ppermute x1, starting transfers between devices, body(): got_even = lax.ppermute(even, LON, pairs_even)  1.92 us
    ppermute x1, starting transfers between devices, body(): got_core = lax.ppermute(core, LAT, pairs_core)  1.92 us
  transfers between devices with their start and end apart: 4, of which 3 were waited for; matrix products, arithmetic and copies ran while one was open for 0% of the time, Pallas kernels for 0%

profile of v1, /device:TPU:1, one launch (start us, length us, event | category | flops | bytes accessed | tf_op | source)
XLA Modules:
  0.0 80.4 jit_solution(9183149971011413391)
XLA Ops:
  0.6 2.9 %sums.1 = (f32[6,8,512]{2,1,0:T(8,128)}, f32[3,8,512]{2,1,0:T(8,128)}, f32[3,8,512]{2,1,0:T(8,128)}) custom-call(f32[40]{0:T(128)} %thick.1, f32[40,8,512]{2,1,0:T(8,128)} %u.1, f32[40,8,512]{2,1,0:T(8,128)} %v.1, f32[8,512]{1,0:T(8,128)} %depth.1, s32[8,512]{1,0:T(8,128)} %mask.1, f32[8,512]{1,0:T(8,128)} %damping.1, f32[8,512]{1,0:T(8,128)} %eta.1), custom_call_target="tpu_custom_call" | custom-call | tf_op jit(solution)/shard_map/sums/pallas_call | solution.py:250
  3.5 24.3 %collective-permute-start = (f32[3,8,512]{2,1,0:T(8,128)}, f32[3,8,512]{2,1,0:T(8,128)S(1)}, u32[]{:S(2)}, u32[]{:S(2)}) collective-permute-start(f32[3,8,512]{2,1,0:T(8,128)} %get-tuple-element.11), channel_id=1, source_target_pairs={{0,1020},{4,8},{8,4},{12,16},{16,12},{20,24},{24,20},{28,32},{32,2... | collective-permute-start | bytes 147464 | tf_op jit(solution)/shard_map/ppermute | solution.py:265
  27.9 1.9 %collective-permute-start.1 = (f32[3,8,512]{2,1,0:T(8,128)}, f32[3,8,512]{2,1,0:T(8,128)S(1)}, u32[]{:S(2)}, u32[]{:S(2)}) collective-permute-start(f32[3,8,512]{2,1,0:T(8,128)} %get-tuple-element.12), channel_id=1, source_target_pairs={{0,4},{4,0},{8,12},{12,8},{16,20},{20,16},{24,28},{28,24},{32,36},... | collective-permute-start | bytes 147464 | tf_op jit(solution)/shard_map/ppermute | solution.py:266
  29.8 0.0 collective-permute-done.got_odd
  29.8 0.0 copy-start.2
  29.8 3.1 %collective-permute-done.1.got_even = f32[3,8,512]{2,1,0:T(8,128)S(1)} collective-permute-done((f32[3,8,512]{2,1,0:T(8,128)}, f32[3,8,512]{2,1,0:T(8,128)S(1)}, u32[]{:S(2)}, u32[]{:S(2)}) %collective-permute-start.1) | collective-permute-done | bytes 49184 | tf_op jit(solution)/shard_map/ppermute | solution.py:266
  32.9 0.0 copy-start.3
  32.9 0.0 copy-done.2
  32.9 0.6 copy-done.3
  33.5 1.6 %join.1 = (f32[6,8,512]{2,1,0:T(8,128)}, f32[12,8,128]{2,1,0:T(8,128)}, f32[12,8,128]{2,1,0:T(8,128)}) custom-call(f32[6,8,512]{2,1,0:T(8,128)} %get-tuple-element.10.own, f32[3,8,512]{2,1,0:T(8,128)} %copy-done.2, f32[3,8,512]{2,1,0:T(8,128)} %copy-done.3), custom_call_target="tpu_custom_call" | custom-call | tf_op jit(solution)/shard_map/join/pallas_call | solution.py:267
  35.2 6.4 %collective-permute-start.2 = (f32[12,8,128]{2,1,0:T(8,128)}, f32[12,8,128]{2,1,0:T(8,128)S(1)}, u32[]{:S(2)}, u32[]{:S(2)}) collective-permute-start(f32[12,8,128]{2,1,0:T(8,128)} %get-tuple-element.14), channel_id=1, source_target_pairs={{1,2},{2,1},{5,6},{6,5},{9,10},{10,9},{13,14},{14,13},{17,18},{18,... | collective-permute-start | bytes 147464 | tf_op jit(solution)/shard_map/ppermute | solution.py:274
  41.6 1.9 %collective-permute-start.3 = (f32[12,8,128]{2,1,0:T(8,128)}, f32[12,8,128]{2,1,0:T(8,128)S(1)}, u32[]{:S(2)}, u32[]{:S(2)}) collective-permute-start(f32[12,8,128]{2,1,0:T(8,128)} %get-tuple-element.15), channel_id=1, source_target_pairs={{0,1},{1,0},{2,3},{3,2},{4,5},{5,4},{6,7},{7,6},{8,9},{9,8},{10,11... | collective-permute-start | bytes 147464 | tf_op jit(solution)/shard_map/ppermute | solution.py:275
  43.5 1.2 %collective-permute-done.2.got_mid = f32[12,8,128]{2,1,0:T(8,128)S(1)} collective-permute-done((f32[12,8,128]{2,1,0:T(8,128)}, f32[12,8,128]{2,1,0:T(8,128)S(1)}, u32[]{:S(2)}, u32[]{:S(2)}) %collective-permute-start.2) | collective-permute-done | bytes 49184 | tf_op jit(solution)/shard_map/ppermute | solution.py:274
  44.7 0.0 copy-start
  44.7 0.2 collective-permute-done.3.got_core
  44.9 0.0 copy-start.1
  44.9 0.4 copy-done
  45.3 0.2 copy-done.1
  45.5 2.0 %basis.1 = (f32[7,8,512]{2,1,0:T(8,128)}, f32[16,128]{1,0:T(8,128)}) custom-call(f32[6,8,512]{2,1,0:T(8,128)} %get-tuple-element.10.own, f32[6,8,512]{2,1,0:T(8,128)} %get-tuple-element.13.halo, f32[12,8,128]{2,1,0:T(8,128)} %copy-done, f32[12,8,128]{2,1,0:T(8,128)} %copy-done.1), custom_call_target="tpu_custom_call" | custom-call | tf_op jit(solution)/shard_map/basis/pallas_call | solution.py:278
  47.5 12.9 %all_to_all.22 = f32[16,1,128]{2,1,0:T(1,128)} all-to-all(f32[16,1,128]{2,1,0:T(1,128)} %bitcast.11), channel_id=1, replica_groups=mesh['lon_0'=8,'lon_1'=8,'lon_2'=4,'lat_0'=2,'lat_1'=2] {'lon_2','lat_0'..., dimensions={0} | all-to-all | bytes 16384 | tf_op jit(solution)/shard_map/all_to_all | solution.py:241
  60.4 1.3 %relay.1 = f32[64,128]{1,0:T(8,128)} custom-call(f32[16,128]{1,0:T(8,128)} %bitcast.10), custom_call_target="tpu_custom_call" | custom-call | tf_op jit(solution)/shard_map/relay/pallas_call | solution.py:286
  61.7 17.0 %all_to_all.23 = f32[64,1,128]{2,1,0:T(1,128)} all-to-all(f32[64,1,128]{2,1,0:T(1,128)} %bitcast.8), channel_id=1, replica_groups=mesh['lon_0'=8,'lon_1'=8,'lon_2'=4,'lat_0'=2,'lat_1'=2] {'lon_0','lon_1'}, dimensions={0} | all-to-all | bytes 65536 | tf_op jit(solution)/shard_map/all_to_all | solution.py:241
  78.7 1.7 %final.1 = (f32[8,512]{1,0:T(8,128)}, f32[8,512]{1,0:T(8,128)}) custom-call(f32[64,128]{1,0:T(8,128)} %bitcast.9, f32[7,8,512]{2,1,0:T(8,128)} %get-tuple-element.17.basis), custom_call_target="tpu_custom_call" | custom-call | tf_op jit(solution)/shard_map/final/pallas_call | solution.py:290
Async XLA Ops:
  3.5 26.3 %collective-permute-start = (f32[3,8,512]{2,1,0:T(8,128)}, f32[3,8,512]{2,1,0:T(8,128)S(1)}, u32[]{:S(2)}, u32[]{:S(2)}) collective-permute-start(f32[3,8,512]{2,1,0:T(8,128)} %get-tuple-element.11), channel_id=1, source_target_pairs={{0,1020},{4,8},{8,4},{12,16},{16,12},{20,24},{24,20},{28,32},{32,2... | collective-permute-start | bytes 147464 | tf_op jit(solution)/shard_map/ppermute | solution.py:265
  27.9 5.0 %collective-permute-start.1 = (f32[3,8,512]{2,1,0:T(8,128)}, f32[3,8,512]{2,1,0:T(8,128)S(1)}, u32[]{:S(2)}, u32[]{:S(2)}) collective-permute-start(f32[3,8,512]{2,1,0:T(8,128)} %get-tuple-element.12), channel_id=1, source_target_pairs={{0,4},{4,0},{8,12},{12,8},{16,20},{20,16},{24,28},{28,24},{32,36},... | collective-permute-start | bytes 147464 | tf_op jit(solution)/shard_map/ppermute | solution.py:266
  29.8 3.1 %copy-start.2 = (f32[3,8,512]{2,1,0:T(8,128)}, f32[3,8,512]{2,1,0:T(8,128)S(1)}, u32[]{:S(2)}) copy-start(f32[3,8,512]{2,1,0:T(8,128)S(1)} %collective-permute-done.got_odd) | copy-start | bytes 147460
  32.9 0.6 copy-start.3
  35.2 9.5 %collective-permute-start.2 = (f32[12,8,128]{2,1,0:T(8,128)}, f32[12,8,128]{2,1,0:T(8,128)S(1)}, u32[]{:S(2)}, u32[]{:S(2)}) collective-permute-start(f32[12,8,128]{2,1,0:T(8,128)} %get-tuple-element.14), channel_id=1, source_target_pairs={{1,2},{2,1},{5,6},{6,5},{9,10},{10,9},{13,14},{14,13},{17,18},{18,... | collective-permute-start | bytes 147464 | tf_op jit(solution)/shard_map/ppermute | solution.py:274
  41.6 3.3 %collective-permute-start.3 = (f32[12,8,128]{2,1,0:T(8,128)}, f32[12,8,128]{2,1,0:T(8,128)S(1)}, u32[]{:S(2)}, u32[]{:S(2)}) collective-permute-start(f32[12,8,128]{2,1,0:T(8,128)} %get-tuple-element.15), channel_id=1, source_target_pairs={{0,1},{1,0},{2,3},{3,2},{4,5},{5,4},{6,7},{7,6},{8,9},{9,8},{10,11... | collective-permute-start | bytes 147464 | tf_op jit(solution)/shard_map/ppermute | solution.py:275
  44.7 0.6 copy-start
  44.9 0.6 copy-start.1

commit v2 on v1

--- a/solution.py
+++ b/solution.py
@@ -21,7 +21,6 @@
 SCALE = 1.0 / math.sqrt(LEVELS)
 VMEM = pl.BlockSpec(memory_space=pltpu.VMEM)
 ANY = pl.BlockSpec(memory_space=pl.ANY)
-SMEM = pl.BlockSpec(memory_space=pltpu.SMEM)
 
 
 def lon_even():
@@ -36,6 +35,10 @@
     return jnp.where(jnp.full(yes.shape, flag), yes, no)
 
 
+def turn(tile, lanes):
+    return tile if lanes % 128 == 0 else pltpu.roll(tile, lanes % 128, 1)
+
+
 def sublane(shape):
     return lax.broadcasted_iota(jnp.int32, shape, len(shape) - 2)
 
@@ -44,8 +47,10 @@
     return lax.broadcasted_iota(jnp.int32, shape, len(shape) - 1)
 
 
-def sum_kernel(thick, u, v, depth, mask, damping, eta, own, odd, even, u_buf, v_buf, f_buf, m_buf, sems, f_sems):
+def sum_kernel(thick_in, u, v, depth, mask, damping, eta, own, odd, even, u_buf, v_buf, f_buf, m_buf, thick, sems, f_sems):
     step = LEVELS // CHUNKS
+    weights = pltpu.make_async_copy(thick_in, thick, f_sems.at[4])
+    weights.start()
     copies = []
     for c in range(CHUNKS):
         part = pl.ds(c * step, step)
@@ -67,6 +72,7 @@
     for s in small:
         s.start()
     total = [jnp.zeros((ROWS, COLS), jnp.float32), jnp.zeros((ROWS, COLS), jnp.float32)]
+    weights.wait()
     for c in range(CHUNKS):
         for i, buf in enumerate((u_buf, v_buf)):
             copies[c][i].wait()
@@ -98,25 +104,31 @@
         below = pick(flag, got_odd[p], got_even[p])
         rows.append(jnp.where(high, below, above))
         rows.append(pltpu.roll(jnp.where(high, above, below), ROWS // 2, 0))
+    spot = lane((ROWS, 128))
+    first = last = jnp.zeros((ROWS, 128), jnp.float32)
     for i in range(FIELDS):
         halo[i] = rows[i]
         for t, tile in enumerate((own[i], rows[i])):
-            first = tile[:, :128]
-            last = tile[:, COLS - 128 :]
-            core[2 * i + t] = pick(side, last, first)
-            mid[2 * i + t] = pick(side, first, last)
+            at = 8 * (2 * i + t)
+            here = jnp.logical_and(spot >= at, spot < at + 4)
+            first = jnp.where(here, turn(tile[:, :128], at), first)
+            last = jnp.where(here, turn(tile[:, COLS - 128 :], at + 4), last)
+    core[...] = pick(side, last, first)
+    mid[...] = pick(side, first, last)
 
 
 def basis_kernel(own, halo, got_mid, got_core, basis, moments):
     side = lat_even()
     right = lane((ROWS, 128)) >= 64
+    above = pick(side, got_core[...], got_mid[...])
+    below = pick(side, got_mid[...], got_core[...])
     fields = []
     for i in range(FIELDS):
         tiles = []
         for t, tile in enumerate((own[i], halo[i])):
-            above = pick(side, got_core[2 * i + t], got_mid[2 * i + t])
-            below = pick(side, got_mid[2 * i + t], got_core[2 * i + t])
-            tiles.append(jnp.concatenate([tile, jnp.where(right, below, above)], axis=1))
+            at = 8 * (2 * i + t)
+            edge = jnp.where(right, turn(below, -at - 4), turn(above, -at))
+            tiles.append(jnp.concatenate([tile, edge], axis=1))
         fields.append(jnp.concatenate(tiles, axis=0))
     sum_east, sum_north, depth, wet, damping, eta = fields
     rows, cols = 2 * ROWS, COLS + 128
@@ -233,8 +245,18 @@
     residual[...] = (pre[0] * basis[3] + pre[1] * basis[4]) + (pre[2] * basis[5] + pre[3] * basis[6])
 
 
+def kept(*dims):
+    return pltpu.VMEM(dims, jnp.float32)
+
+
 def shape(*dims):
     return jax.ShapeDtypeStruct(dims, jnp.float32)
+
+
+def call(kernel, name, outs, *args):
+    args = [pltpu.with_memory_space_constraint(a, pltpu.VMEM) for a in args]
+    specs = jax.tree.map(lambda _: VMEM, outs)
+    return pl.pallas_call(kernel, out_shape=outs, in_specs=[VMEM] * len(args), out_specs=specs, name=name)(*args)
 
 
 def total_over(rows, axes):
@@ -249,51 +271,32 @@
     pairs_mid = [(1, 2), (2, 1)]
     own, odd, even = pl.pallas_call(
         sum_kernel,
-        out_shape=(shape(FIELDS, ROWS, COLS), shape(3, ROWS, COLS), shape(3, ROWS, COLS)),
-        in_specs=[SMEM] + [ANY] * 6,
+        out_shape=(kept(FIELDS, ROWS, COLS), kept(3, ROWS, COLS), kept(3, ROWS, COLS)),
+        in_specs=[ANY] * 7,
         out_specs=(VMEM, VMEM, VMEM),
         scratch_shapes=[
             pltpu.VMEM((LEVELS, ROWS, COLS), jnp.float32),
             pltpu.VMEM((LEVELS, ROWS, COLS), jnp.float32),
             pltpu.VMEM((3, ROWS, COLS), jnp.float32),
             pltpu.VMEM((ROWS, COLS), jnp.int32),
+            pltpu.SMEM((LEVELS,), jnp.float32),
             pltpu.SemaphoreType.DMA((2, CHUNKS)),
-            pltpu.SemaphoreType.DMA((4,)),
+            pltpu.SemaphoreType.DMA((5,)),
         ],
         name="sums",
     )(thickness, u_vel, v_vel, depth, sea_mask, damping, eta_prev)
     got_odd = lax.ppermute(odd, LON, pairs_odd)
     got_even = lax.ppermute(even, LON, pairs_even)
-    halo, mid, core = pl.pallas_call(
-        join_kernel,
-        out_shape=(shape(FIELDS, ROWS, COLS), shape(12, ROWS, 128), shape(12, ROWS, 128)),
-        in_specs=[VMEM] * 3,
-        out_specs=(VMEM,) * 3,
-        name="join",
-    )(own, got_odd, got_even)
+    outs = (kept(FIELDS, ROWS, COLS), kept(ROWS, 128), kept(ROWS, 128))
+    halo, mid, core = call(join_kernel, "join", outs, own, got_odd, got_even)
     got_mid = lax.ppermute(mid, LAT, pairs_mid)
     got_core = lax.ppermute(core, LAT, pairs_core)
-    near = lax.axis_size(NEAR)
-    far = lax.axis_size(FAR)
-    basis, moments = pl.pallas_call(
-        basis_kernel,
-        out_shape=(shape(7, ROWS, COLS), shape(near, 128)),
-        in_specs=[VMEM] * 4,
-        out_specs=(VMEM,) * 2,
-        name="basis",
-    )(own, halo, got_mid, got_core)
+    outs = (kept(7, ROWS, COLS), kept(lax.axis_size(NEAR), 128))
+    basis, moments = call(basis_kernel, "basis", outs, own, halo, got_mid, got_core)
     moments = total_over(moments, NEAR)
-    moments = pl.pallas_call(
-        relay_kernel, out_shape=shape(far, 128), in_specs=[VMEM], out_specs=VMEM, name="relay"
-    )(moments)
+    moments = call(relay_kernel, "relay", kept(lax.axis_size(FAR), 128), moments)
     moments = total_over(moments, FAR)
-    return pl.pallas_call(
-        final_kernel,
-        out_shape=(shape(ROWS, COLS), shape(ROWS, COLS)),
-        in_specs=[VMEM] * 2,
-        out_specs=(VMEM,) * 2,
-        name="final",
-    )(moments, basis)
+    return call(final_kernel, "final", (shape(ROWS, COLS), shape(ROWS, COLS)), moments, basis)
 
 
 def solution(mesh):

time: 80.8 us -> 71.6 us (0.89)
  Pallas kernels: 9.53 us -> 2.98 us
  local copies, waits for them, and re-layouts: 1.23 us -> 0 us
  blocking collectives: 29.9 us -> 29 us
    pallas_call x5, Pallas kernels: 9.53 us -> 2.98 us  [the longest x1 1.58 us: body(): pl.pallas_call(sum_kernel, out_shape=(kept(FIELDS, ROWS, COLS), kept(3, R...]
    unnamed x8 -> x0, local copies, waits for them, and re-layouts: 1.23 us -> none
    all_to_all x2, blocking collectives: 29.9 us -> 29 us  [total_over(): return lax.all_to_all(rows, axes, 0, 0, tiled=True)]
where the time goes in v2:
time: 71.6 us; the launch traced here: 71.3 us
  starting transfers between devices  34.6 us (48%)
  blocking collectives  29 us (41%)
  waiting for transfers between devices  4.03 us (6%)
  Pallas kernels  2.98 us (4%)
    all_to_all x2, blocking collectives, total_over(): return lax.all_to_all(rows, axes, 0, 0, tiled=True)  29 us
    ppermute x1, starting transfers between devices, body(): got_odd = lax.ppermute(odd, LON, pairs_odd)  24.3 us
    ppermute x1, starting transfers between devices, body(): got_mid = lax.ppermute(mid, LAT, pairs_mid)  6.41 us
    ppermute x1, waiting for transfers between devices, body(): got_even = lax.ppermute(even, LON, pairs_even)  2.9 us
    ppermute x1, starting transfers between devices, body(): got_even = lax.ppermute(even, LON, pairs_even)  1.92 us
    ppermute x1, starting transfers between devices, body(): got_core = lax.ppermute(core, LAT, pairs_core)  1.92 us
    pallas_call x1, Pallas kernels, body(): pl.pallas_call(sum_kernel, out_shape=(kept(FIELDS, ROWS, COLS), kept(3, R...  1.58 us
  transfers between devices with their start and end apart: 4, of which 3 were waited for; matrix products, arithmetic and copies ran while one was open for 0% of the time, Pallas kernels for 0%

profile of v2, /device:TPU:1, one launch (start us, length us, event | category | flops | bytes accessed | tf_op | source)
XLA Modules:
  0.0 71.3 jit_solution(10583956771168682676)
XLA Ops:
  0.6 1.6 %sums.1 = (f32[6,8,512]{2,1,0:T(8,128)S(1)}, f32[3,8,512]{2,1,0:T(8,128)S(1)}, f32[3,8,512]{2,1,0:T(8,128)S(1)}) custom-call(f32[40]{0:T(128)} %thick_in.1, f32[40,8,512]{2,1,0:T(8,128)} %u.1, f32[40,8,512]{2,1,0:T(8,128)} %v.1, f32[8,512]{1,0:T(8,128)} %depth.1, s32[8,512]{1,0:T(8,128)} %mask.1, f32[8,512]{1,0:T(8,128)} %damping.1, f32[8,512]{1,0:T(8,128)} %eta.1), custom_call_target="tpu_custom_call" | custom-call | tf_op jit(solution)/shard_map/sums/pallas_call | solution.py:272
  2.2 24.3 %collective-permute-start = (f32[3,8,512]{2,1,0:T(8,128)S(1)}, f32[3,8,512]{2,1,0:T(8,128)S(1)}, u32[]{:S(2)}, u32[]{:S(2)}) collective-permute-start(f32[3,8,512]{2,1,0:T(8,128)S(1)} %get-tuple-element.11), channel_id=1, source_target_pairs={{0,1020},{4,8},{8,4},{12,16},{16,12},{20,24},{24,20},{28,32},{32,2... | collective-permute-start | bytes 147464 | tf_op jit(solution)/shard_map/ppermute | solution.py:288
  26.6 1.9 %collective-permute-start.1 = (f32[3,8,512]{2,1,0:T(8,128)S(1)}, f32[3,8,512]{2,1,0:T(8,128)S(1)}, u32[]{:S(2)}, u32[]{:S(2)}) collective-permute-start(f32[3,8,512]{2,1,0:T(8,128)S(1)} %get-tuple-element.12), channel_id=1, source_target_pairs={{0,4},{4,0},{8,12},{12,8},{16,20},{20,16},{24,28},{28,24},{32,36},... | collective-permute-start | bytes 147464 | tf_op jit(solution)/shard_map/ppermute | solution.py:289
  28.5 0.0 collective-permute-done.got_odd
  28.5 2.9 %collective-permute-done.1.got_even = f32[3,8,512]{2,1,0:T(8,128)S(1)} collective-permute-done((f32[3,8,512]{2,1,0:T(8,128)S(1)}, f32[3,8,512]{2,1,0:T(8,128)S(1)}, u32[]{:S(2)}, u32[]{:S(2)}) %collective-permute-start.1) | collective-permute-done | bytes 49184 | tf_op jit(solution)/shard_map/ppermute | solution.py:289
  31.4 0.1 join.1
  31.5 6.4 %collective-permute-start.2 = (f32[8,128]{1,0:T(8,128)S(1)}, f32[8,128]{1,0:T(8,128)S(1)}, u32[]{:S(2)}, u32[]{:S(2)}) collective-permute-start(f32[8,128]{1,0:T(8,128)S(1)} %get-tuple-element.14), channel_id=1, source_target_pairs={{1,2},{2,1},{5,6},{6,5},{9,10},{10,9},{13,14},{14,13},{17,18},{18,... | collective-permute-start | bytes 12296 | tf_op jit(solution)/shard_map/ppermute | solution.py:292
  37.9 1.9 %collective-permute-start.3 = (f32[8,128]{1,0:T(8,128)S(1)}, f32[8,128]{1,0:T(8,128)S(1)}, u32[]{:S(2)}, u32[]{:S(2)}) collective-permute-start(f32[8,128]{1,0:T(8,128)S(1)} %get-tuple-element.15), channel_id=1, source_target_pairs={{0,1},{1,0},{2,3},{3,2},{4,5},{5,4},{6,7},{7,6},{8,9},{9,8},{10,11... | collective-permute-start | bytes 12296 | tf_op jit(solution)/shard_map/ppermute | solution.py:293
  39.8 0.5 collective-permute-done.2.got_mid
  40.3 0.6 collective-permute-done.3.got_core
  41.0 0.5 basis.1
  41.5 12.4 %all_to_all.22 = f32[16,1,128]{2,1,0:T(1,128)S(1)} all-to-all(f32[16,1,128]{2,1,0:T(1,128)S(1)} %bitcast.11), channel_id=1, replica_groups=mesh['lon_0'=8,'lon_1'=8,'lon_2'=4,'lat_0'=2,'lat_1'=2] {'lon_2','lat_0'..., dimensions={0} | all-to-all | bytes 16384 | tf_op jit(solution)/shard_map/all_to_all | solution.py:263
  53.9 16.6 %all_to_all.23 = f32[64,1,128]{2,1,0:T(1,128)S(1)} all-to-all(f32[64,1,128]{2,1,0:T(1,128)S(1)} %bitcast.8), channel_id=1, replica_groups=mesh['lon_0'=8,'lon_1'=8,'lon_2'=4,'lat_0'=2,'lat_1'=2] {'lon_0','lon_1'}, dimensions={0} | all-to-all | bytes 65536 | tf_op jit(solution)/shard_map/all_to_all | solution.py:263
  70.5 0.8 %final.1 = (f32[8,512]{1,0:T(8,128)}, f32[8,512]{1,0:T(8,128)}) custom-call(f32[64,128]{1,0:T(8,128)S(1)} %bitcast.9, f32[7,8,512]{2,1,0:T(8,128)S(1)} %get-tuple-element.17.basis), custom_call_target="tpu_custom_call" | custom-call | tf_op jit(solution)/shard_map/final/pallas_call | solution.py:259
  (1 shorter events, 0.0 us)
Async XLA Ops:
  2.2 26.3 %collective-permute-start = (f32[3,8,512]{2,1,0:T(8,128)S(1)}, f32[3,8,512]{2,1,0:T(8,128)S(1)}, u32[]{:S(2)}, u32[]{:S(2)}) collective-permute-start(f32[3,8,512]{2,1,0:T(8,128)S(1)} %get-tuple-element.11), channel_id=1, source_target_pairs={{0,1020},{4,8},{8,4},{12,16},{16,12},{20,24},{24,20},{28,32},{32,2... | collective-permute-start | bytes 147464 | tf_op jit(solution)/shard_map/ppermute | solution.py:288
  26.6 4.8 %collective-permute-start.1 = (f32[3,8,512]{2,1,0:T(8,128)S(1)}, f32[3,8,512]{2,1,0:T(8,128)S(1)}, u32[]{:S(2)}, u32[]{:S(2)}) collective-permute-start(f32[3,8,512]{2,1,0:T(8,128)S(1)} %get-tuple-element.12), channel_id=1, source_target_pairs={{0,4},{4,0},{8,12},{12,8},{16,20},{20,16},{24,28},{28,24},{32,36},... | collective-permute-start | bytes 147464 | tf_op jit(solution)/shard_map/ppermute | solution.py:289
  31.5 8.8 %collective-permute-start.2 = (f32[8,128]{1,0:T(8,128)S(1)}, f32[8,128]{1,0:T(8,128)S(1)}, u32[]{:S(2)}, u32[]{:S(2)}) collective-permute-start(f32[8,128]{1,0:T(8,128)S(1)} %get-tuple-element.14), channel_id=1, source_target_pairs={{1,2},{2,1},{5,6},{6,5},{9,10},{10,9},{13,14},{14,13},{17,18},{18,... | collective-permute-start | bytes 12296 | tf_op jit(solution)/shard_map/ppermute | solution.py:292
  37.9 3.1 %collective-permute-start.3 = (f32[8,128]{1,0:T(8,128)S(1)}, f32[8,128]{1,0:T(8,128)S(1)}, u32[]{:S(2)}, u32[]{:S(2)}) collective-permute-start(f32[8,128]{1,0:T(8,128)S(1)} %get-tuple-element.15), channel_id=1, source_target_pairs={{0,1},{1,0},{2,3},{3,2},{4,5},{5,4},{6,7},{7,6},{8,9},{9,8},{10,11... | collective-permute-start | bytes 12296 | tf_op jit(solution)/shard_map/ppermute | solution.py:293

commit v3 on v2

--- a/solution.py
+++ b/solution.py
@@ -1,4 +1,3 @@
-import functools
 import math
 
 import jax
@@ -14,6 +13,11 @@
 ROWS = 8
 COLS = 512
 FIELDS = 6
+REACH = 4
+WIDTH = 7
+EDGE = 112
+MOMENTS = 122
+EDGE_COLS = 256
 LON = ("lon_0", "lon_1", "lon_2")
 LAT = ("lat_0", "lat_1")
 NEAR = ("lon_2", "lat_0", "lat_1")
@@ -27,8 +31,8 @@
     return lax.rem(lax.axis_index("lon_2"), 2) == 0
 
 
-def lat_even():
-    return lax.axis_index("lat_1") == 0
+def lat_index():
+    return 2 * lax.axis_index("lat_0") + lax.axis_index("lat_1")
 
 
 def pick(flag, yes, no):
@@ -94,9 +98,41 @@
         odd[p] = pick(flag, first, last)
 
 
-def join_kernel(own, got_odd, got_even, halo, mid, core):
+def stencil(face_x, face_y, rhs, diag):
+    rows, cols = rhs.shape
+    back_x, back_y = pltpu.roll(face_x, 1, 0), pltpu.roll(face_y, 1, 1)
+    diag = jnp.where(diag > 0.0, diag, 1.0)
+
+    def spread(a):
+        ends = face_x * pltpu.roll(a, rows - 1, 0) + back_x * pltpu.roll(a, 1, 0)
+        return ends + face_y * pltpu.roll(a, cols - 1, 1) + back_y * pltpu.roll(a, 1, 1)
+
+    w0 = rhs
+    v0 = w0 / diag
+    w1 = spread(v0)
+    v1 = w1 / diag
+    w2 = spread(v1)
+    v2 = w2 / diag
+    w3 = spread(v2)
+    return [a[:ROWS] for a in (v0, v1, v2, w0, w1, w2, w3)]
+
+
+def add_moments(basis, keep, first):
+    v0, v1, v2, w0, w1, w2, w3 = basis
+    row = jnp.zeros((1, 128), jnp.float32)
+    spot = lane((1, 128))
+    for k, (a, b) in enumerate(((v0, w0), (v0, w1), (v1, w1), (v1, w2), (v2, w2), (v2, w3))):
+        prod = jnp.where(keep, a * b, 0.0)
+        tiles = [prod[:, i : i + 128] for i in range(0, prod.shape[1], 128)]
+        while len(tiles) > 1:
+            tiles = [tiles[i] + tiles[i + 1] for i in range(0, len(tiles), 2)]
+        total = jnp.sum(jnp.sum(tiles[0], axis=0, keepdims=True), axis=1, keepdims=True)
+        row = jnp.where(spot == first + k, total, row)
+    return row
+
+
+def block_kernel(own, got_odd, got_even, basis, slots):
     flag = lon_even()
-    side = lat_even()
     high = sublane((ROWS, COLS)) >= ROWS // 2
     rows = []
     for p in range(FIELDS // 2):
@@ -104,88 +140,90 @@
         below = pick(flag, got_odd[p], got_even[p])
         rows.append(jnp.where(high, below, above))
         rows.append(pltpu.roll(jnp.where(high, above, below), ROWS // 2, 0))
-    spot = lane((ROWS, 128))
-    first = last = jnp.zeros((ROWS, 128), jnp.float32)
-    for i in range(FIELDS):
-        halo[i] = rows[i]
-        for t, tile in enumerate((own[i], rows[i])):
-            at = 8 * (2 * i + t)
-            here = jnp.logical_and(spot >= at, spot < at + 4)
-            first = jnp.where(here, turn(tile[:, :128], at), first)
-            last = jnp.where(here, turn(tile[:, COLS - 128 :], at + 4), last)
-    core[...] = pick(side, last, first)
-    mid[...] = pick(side, first, last)
-
-
-def basis_kernel(own, halo, got_mid, got_core, basis, moments):
-    side = lat_even()
-    right = lane((ROWS, 128)) >= 64
-    above = pick(side, got_core[...], got_mid[...])
-    below = pick(side, got_mid[...], got_core[...])
-    fields = []
-    for i in range(FIELDS):
-        tiles = []
-        for t, tile in enumerate((own[i], halo[i])):
-            at = 8 * (2 * i + t)
-            edge = jnp.where(right, turn(below, -at - 4), turn(above, -at))
-            tiles.append(jnp.concatenate([tile, edge], axis=1))
-        fields.append(jnp.concatenate(tiles, axis=0))
+    fields = [jnp.concatenate([own[i], rows[i]], axis=0) for i in range(FIELDS)]
     sum_east, sum_north, depth, wet, damping, eta = fields
-    rows, cols = 2 * ROWS, COLS + 128
-
-    def east(a):
-        return pltpu.roll(a, rows - 1, 0)
-
-    def west(a):
-        return pltpu.roll(a, 1, 0)
-
-    def north(a):
-        return pltpu.roll(a, cols - 1, 1)
-
-    def south(a):
-        return pltpu.roll(a, 1, 1)
-
-    wet_x = wet * east(wet)
-    wet_y = wet * north(wet)
-    face_x = wet_x * 0.5 * (depth + east(depth))
-    face_y = wet_y * 0.5 * (depth + north(depth))
+    inner = lane(wet.shape) < COLS - 1
+    wet_x = wet * pltpu.roll(wet, 2 * ROWS - 1, 0)
+    wet_y = jnp.where(inner, wet * pltpu.roll(wet, COLS - 1, 1), 0.0)
+    face_x = wet_x * 0.5 * (depth + pltpu.roll(depth, 2 * ROWS - 1, 0))
+    face_y = wet_y * 0.5 * (depth + pltpu.roll(depth, COLS - 1, 1))
     flux_x = wet_x * sum_east
     flux_y = wet_y * sum_north
-    diverge = flux_x - west(flux_x) + flux_y - south(flux_y)
+    diverge = flux_x - pltpu.roll(flux_x, 1, 0) + flux_y - pltpu.roll(flux_y, 1, 1)
     rhs = wet * (damping * eta - diverge)
-    back_x, back_y = west(face_x), south(face_y)
-    diag = damping + face_x + back_x + face_y + back_y
-    diag = jnp.where(diag > 0.0, diag, 1.0)
-
-    def spread(a):
-        return face_x * east(a) + back_x * west(a) + face_y * north(a) + back_y * south(a)
-
-    def mine(a):
-        return a[:ROWS, :COLS]
-
-    w0 = rhs
-    v0 = w0 / diag
-    w1 = spread(v0)
-    v1 = w1 / diag
-    w2 = spread(v1)
-    v2 = w2 / diag
-    w3 = spread(v2)
-    parts = [mine(a) for a in (v0, v1, v2, w0, w1, w2, w3)]
+    diag = damping + face_x + pltpu.roll(face_x, 1, 0) + face_y + pltpu.roll(face_y, 1, 1)
+    parts = stencil(face_x, face_y, rhs, diag)
     for i, part in enumerate(parts):
         basis[i] = part
-    v0, v1, v2, w0, w1, w2, w3 = parts
-    row = jnp.zeros((1, 128), jnp.float32)
-    spot = lane((1, 128))
-    for k, (a, b) in enumerate(((v0, w0), (v0, w1), (v1, w1), (v1, w2), (v2, w2), (v2, w3))):
-        prod = a * b
-        prod = prod[:, :128] + prod[:, 128:256] + (prod[:, 256:384] + prod[:, 384:])
-        total = jnp.sum(jnp.sum(prod, axis=0, keepdims=True), axis=1, keepdims=True)
-        row = jnp.where(spot == k, total, row)
-    moments[...] = jnp.broadcast_to(row, moments.shape)
-
-
-def relay_kernel(parts, out):
-    out[...] = jnp.broadcast_to(jnp.sum(parts[...], axis=0, keepdims=True), out.shape)
+    place = lat_index()
+    spot = lane((ROWS, COLS))
+    low = jnp.where(place == 0, 0, REACH)
+    top = jnp.where(place == lax.axis_size(LAT) - 1, COLS, COLS - REACH)
+    keep = jnp.logical_and(spot >= low, spot < top)
+    row = add_moments(parts, keep, MOMENTS)
+    spot = lane((ROWS, 128))
+    tile = jnp.where(sublane((ROWS, 128)) == 0, row, 0.0)
+    pieces = []
+    for t in range(2):
+        for i, field in enumerate((rhs, diag, face_x, face_y)):
+            at = 2 * WIDTH * (4 * t + i)
+            pieces.append((field, t, COLS - WIDTH, at, WIDTH))
+            pieces.append((field, t, 0, at + WIDTH, WIDTH))
+        for i, field in enumerate((wet, depth, sum_north)):
+            pieces.append((field, t, COLS - 1, EDGE + 2 * i + t, 1))
+        for i, field in enumerate((wet, depth)):
+            pieces.append((field, t, 0, EDGE + 6 + 2 * i + t, 1))
+    for field, t, start, at, size in pieces:
+        base = start - start % 128
+        moved = turn(field[ROWS * t : ROWS * (t + 1), base : base + 128], at - start % 128)
+        tile = jnp.where(jnp.logical_and(spot >= at, spot < at + size), moved, tile)
+    for i in range(slots.shape[0]):
+        slots[i] = tile
+
+
+def edge_kernel(slots, edge_basis, moments):
+    spot = lane((ROWS, 128))
+    count = lax.axis_size(LAT)
+    group = slots.shape[0]
+    left = jnp.logical_and(spot < EDGE, lax.rem(spot, 2 * WIDTH) < WIDTH)
+    left = jnp.logical_or(left, jnp.logical_and(spot >= EDGE, spot < EDGE + 6))
+    tiles = EDGE_COLS // 128
+    zero = jnp.zeros((ROWS, 128), jnp.float32)
+    fields = [[[zero for _ in range(tiles)] for _ in range(2)] for _ in range(6)]
+    for b in range(group // count * (count - 1)):
+        slot = b // (count - 1) * count + b % (count - 1)
+        pair = jnp.where(left, slots[slot], slots[slot + 1])
+        far = turn(pair, -6)
+        wets = pair * far
+        face = wets * 0.5 * turn(pair + far, -2)
+        flux = wets * turn(pair, -4)
+        at, home = 16 * (b % 8), b // 8
+        here = jnp.logical_and(spot >= at, spot < at + 2 * WIDTH)
+        seam = spot == at + WIDTH - 1
+        for t in range(2):
+            for i in range(4):
+                moved = turn(pair, at - 2 * WIDTH * (4 * t + i))
+                fields[i][t][home] = jnp.where(here, moved, fields[i][t][home])
+            for i, value in enumerate((face, flux)):
+                moved = turn(value, at + WIDTH - 1 - EDGE - t)
+                fields[4 + i][t][home] = jnp.where(seam, moved, fields[4 + i][t][home])
+    fields = [jnp.concatenate([jnp.concatenate(f[t], axis=1) for t in range(2)], axis=0) for f in fields]
+    rhs, diag, face_x, face_y, face, flux = fields
+    rhs = rhs - flux + pltpu.roll(flux, 1, 1)
+    diag = diag + face + pltpu.roll(face, 1, 1)
+    face_y = face_y + face
+    parts = stencil(face_x, face_y, rhs, diag)
+    for i, part in enumerate(parts):
+        edge_basis[i] = part
+    spot = lane((ROWS, EDGE_COLS))
+    column = lax.rem(spot, 16)
+    keep = jnp.logical_and(column >= WIDTH - REACH, column < WIDTH + REACH)
+    row = add_moments(parts, keep, MOMENTS)
+    total = slots[0]
+    for i in range(1, group):
+        total = total + slots[i]
+    total = total[:1] + row
+    moments[...] = jnp.broadcast_to(total, moments.shape)
 
 
 def poly(a, b, scale):
@@ -215,10 +253,10 @@
     return total
 
 
-def final_kernel(parts, basis, surface, residual):
+def final_kernel(parts, basis, edge_basis, surface, residual):
     row = jnp.sum(parts[...], axis=0, keepdims=True)
     spot = lane((1, 128))
-    moments = [jnp.sum(jnp.where(spot == k, row, 0.0), axis=1, keepdims=True) for k in range(6)]
+    moments = [jnp.sum(jnp.where(spot == MOMENTS + k, row, 0.0), axis=1, keepdims=True) for k in range(6)]
     one = jnp.ones((1, 1), jnp.float32)
     gaps = [moments[k] - moments[k + 1] for k in range(5)]
     pre = [one]
@@ -241,8 +279,26 @@
         direction = poly(pre, direction, ratio)
         answer = poly(answer, direction, step)
         gamma = gamma_next
-    surface[...] = answer[0] * basis[0] + answer[1] * basis[1] + answer[2] * basis[2]
-    residual[...] = (pre[0] * basis[3] + pre[1] * basis[4]) + (pre[2] * basis[5] + pre[3] * basis[6])
+
+    def combine(b):
+        eta = answer[0] * b[0] + answer[1] * b[1] + answer[2] * b[2]
+        return eta, (pre[0] * b[3] + pre[1] * b[4]) + (pre[2] * b[5] + pre[3] * b[6])
+
+    inner, edge = combine(basis), combine(edge_basis)
+    place, count = lat_index(), lax.axis_size(LAT)
+    group = lax.axis_index("lon_2") * (count - 1)
+    spot = lane((ROWS, 128))
+    for out, body, strip in ((surface, inner[0], edge[0]), (residual, inner[1], edge[1])):
+        out[:, 128 : COLS - 128] = body[:, 128 : COLS - 128]
+        for side, ok, base, near in ((-1, place > 0, 0, spot < REACH), (0, place < count - 1, COLS - 128, spot >= 128 - REACH)):
+            b = group + place + side
+            tile = strip[:, :128]
+            for i in range(1, EDGE_COLS // 128):
+                tile = pick(b // 8 == i, strip[:, 128 * i : 128 * (i + 1)], tile)
+            start = 16 * lax.rem(b, 8) + WIDTH
+            moved = pltpu.roll(tile, lax.rem(256 - start, 128), 1)
+            use = jnp.logical_and(near, ok)
+            out[:, base : base + 128] = jnp.where(use, moved, body[:, base : base + 128])
 
 
 def kept(*dims):
@@ -259,16 +315,10 @@
     return pl.pallas_call(kernel, out_shape=outs, in_specs=[VMEM] * len(args), out_specs=specs, name=name)(*args)
 
 
-def total_over(rows, axes):
-    return lax.all_to_all(rows, axes, 0, 0, tiled=True)
-
-
 def body(u_vel, v_vel, thickness, depth, sea_mask, damping, eta_prev):
     count = lax.axis_size(LON)
     pairs_even = [(i, i ^ 1) for i in range(count)]
     pairs_odd = [(i, (i + 1) % count) if i % 2 else (i, (i - 1) % count) for i in range(count)]
-    pairs_core = [(0, 1), (1, 0), (2, 3), (3, 2)]
-    pairs_mid = [(1, 2), (2, 1)]
     own, odd, even = pl.pallas_call(
         sum_kernel,
         out_shape=(kept(FIELDS, ROWS, COLS), kept(3, ROWS, COLS), kept(3, ROWS, COLS)),
@@ -287,16 +337,13 @@
     )(thickness, u_vel, v_vel, depth, sea_mask, damping, eta_prev)
     got_odd = lax.ppermute(odd, LON, pairs_odd)
     got_even = lax.ppermute(even, LON, pairs_even)
-    outs = (kept(FIELDS, ROWS, COLS), kept(ROWS, 128), kept(ROWS, 128))
-    halo, mid, core = call(join_kernel, "join", outs, own, got_odd, got_even)
-    got_mid = lax.ppermute(mid, LAT, pairs_mid)
-    got_core = lax.ppermute(core, LAT, pairs_core)
-    outs = (kept(7, ROWS, COLS), kept(lax.axis_size(NEAR), 128))
-    basis, moments = call(basis_kernel, "basis", outs, own, halo, got_mid, got_core)
-    moments = total_over(moments, NEAR)
-    moments = call(relay_kernel, "relay", kept(lax.axis_size(FAR), 128), moments)
-    moments = total_over(moments, FAR)
-    return call(final_kernel, "final", (shape(ROWS, COLS), shape(ROWS, COLS)), moments, basis)
+    near, far = lax.axis_size(NEAR), lax.axis_size(FAR)
+    basis, slots = call(block_kernel, "block", (kept(7, ROWS, COLS), kept(near, ROWS, 128)), own, got_odd, got_even)
+    slots = lax.all_to_all(slots, NEAR, 0, 0, tiled=True)
+    edge_basis, moments = call(edge_kernel, "edge", (kept(7, ROWS, EDGE_COLS), kept(far, 128)), slots)
+    moments = lax.all_to_all(moments, FAR, 0, 0, tiled=True)
+    outs = (shape(ROWS, COLS), shape(ROWS, COLS))
+    return call(final_kernel, "final", outs, moments, basis, edge_basis)
 
 
 def solution(mesh):

time: 71.6 us -> 64 us (0.89)
  starting transfers between devices: 34.6 us -> 26.3 us
  blocking collectives: 29 us -> 30.4 us
  waiting for transfers between devices: 4.03 us -> 2.9 us
    ppermute x2 -> x0, starting transfers between devices: 8.33 us -> none  [the longest x1 6.41 us: body(): got_mid = lax.ppermute(mid, LAT, pairs_mid)]
    all_to_all x2, blocking collectives: 29 us -> 30.4 us  [the longest x1 16.6 us: body(): moments = lax.all_to_all(moments, FAR, 0, 0, tiled=True)]
    ppermute x2 -> x0, waiting for transfers between devices: 1.13 us -> none  [the longest x1 0.64 us: body(): got_core = lax.ppermute(core, LAT, pairs_core)]
    pallas_call x4 -> x3, Pallas kernels: 1.4 us -> 1.95 us  [call(): pl.pallas_call(kernel, out_shape=outs, in_specs=[VMEM] * len(args), out_s...]
  transfers between devices with their start and end apart: 4 -> 2, of which waited for: 3 -> 1; matrix products, arithmetic and copies ran while one was open for 0% -> 0% of each run, Pallas kernels for 0% -> 0%
where the time goes in v3:
time: 64 us; the launch traced here: 63.8 us
  blocking collectives  30.4 us (48%)
  starting transfers between devices  26.3 us (41%)
  Pallas kernels  3.53 us (6%)
  waiting for transfers between devices  2.9 us (5%)
  between operations  0.67 us (1%)
    ppermute x1, starting transfers between devices, body(): got_odd = lax.ppermute(odd, LON, pairs_odd)  24.3 us
    all_to_all x1, blocking collectives, body(): moments = lax.all_to_all(moments, FAR, 0, 0, tiled=True)  16.6 us
    all_to_all x1, blocking collectives, body(): slots = lax.all_to_all(slots, NEAR, 0, 0, tiled=True)  13.8 us
    ppermute x1, waiting for transfers between devices, body(): got_even = lax.ppermute(even, LON, pairs_even)  2.9 us
    pallas_call x3, Pallas kernels, call(): pl.pallas_call(kernel, out_shape=outs, in_specs=[VMEM] * len(args), out_s...  1.95 us
    ppermute x1, starting transfers between devices, body(): got_even = lax.ppermute(even, LON, pairs_even)  1.92 us
    pallas_call x1, Pallas kernels, body(): pl.pallas_call(sum_kernel, out_shape=(kept(FIELDS, ROWS, COLS), kept(3, R...  1.58 us
  transfers between devices with their start and end apart: 2, of which 1 were waited for; matrix products, arithmetic and copies ran while one was open for 0% of the time, Pallas kernels for 0%

profile of v3, /device:TPU:1, one launch (start us, length us, event | category | flops | bytes accessed | tf_op | source)
XLA Modules:
  0.0 63.8 jit_solution(10490710969547989235)
XLA Ops:
  0.6 1.6 %sums.1 = (f32[6,8,512]{2,1,0:T(8,128)S(1)}, f32[3,8,512]{2,1,0:T(8,128)S(1)}, f32[3,8,512]{2,1,0:T(8,128)S(1)}) custom-call(f32[40]{0:T(128)} %thick_in.1, f32[40,8,512]{2,1,0:T(8,128)} %u.1, f32[40,8,512]{2,1,0:T(8,128)} %v.1, f32[8,512]{1,0:T(8,128)} %depth.1, s32[8,512]{1,0:T(8,128)} %mask.1, f32[8,512]{1,0:T(8,128)} %damping.1, f32[8,512]{1,0:T(8,128)} %eta.1), custom_call_target="tpu_custom_call" | custom-call | tf_op jit(solution)/shard_map/sums/pallas_call | solution.py:322
  2.2 24.3 %collective-permute-start = (f32[3,8,512]{2,1,0:T(8,128)S(1)}, f32[3,8,512]{2,1,0:T(8,128)S(1)}, u32[]{:S(2)}, u32[]{:S(2)}) collective-permute-start(f32[3,8,512]{2,1,0:T(8,128)S(1)} %get-tuple-element.10), channel_id=1, source_target_pairs={{0,1020},{4,8},{8,4},{12,16},{16,12},{20,24},{24,20},{28,32},{32,2... | collective-permute-start | bytes 147464 | tf_op jit(solution)/shard_map/ppermute | solution.py:338
  26.6 1.9 %collective-permute-start.1 = (f32[3,8,512]{2,1,0:T(8,128)S(1)}, f32[3,8,512]{2,1,0:T(8,128)S(1)}, u32[]{:S(2)}, u32[]{:S(2)}) collective-permute-start(f32[3,8,512]{2,1,0:T(8,128)S(1)} %get-tuple-element.11), channel_id=1, source_target_pairs={{0,4},{4,0},{8,12},{12,8},{16,20},{20,16},{24,28},{28,24},{32,36},... | collective-permute-start | bytes 147464 | tf_op jit(solution)/shard_map/ppermute | solution.py:339
  28.5 0.0 collective-permute-done.got_odd
  28.5 2.9 %collective-permute-done.1.got_even = f32[3,8,512]{2,1,0:T(8,128)S(1)} collective-permute-done((f32[3,8,512]{2,1,0:T(8,128)S(1)}, f32[3,8,512]{2,1,0:T(8,128)S(1)}, u32[]{:S(2)}, u32[]{:S(2)}) %collective-permute-start.1) | collective-permute-done | bytes 49184 | tf_op jit(solution)/shard_map/ppermute | solution.py:339
  31.4 0.5 block.1
  31.9 13.8 %all_to_all.16.slots = f32[16,8,128]{2,1,0:T(8,128)S(1)} all-to-all(f32[16,8,128]{2,1,0:T(8,128)S(1)} %get-tuple-element.12), channel_id=1, replica_groups=mesh['lon_0'=8,'lon_1'=8,'lon_2'=4,'lat_0'=2,'lat_1'=2] {'lon_2','lat_0'..., dimensions={0} | all-to-all | bytes 131072 | tf_op jit(solution)/shard_map/all_to_all | solution.py:342
  45.7 0.6 edge.1
  46.3 16.6 %all_to_all.17 = f32[64,1,128]{2,1,0:T(1,128)S(1)} all-to-all(f32[64,1,128]{2,1,0:T(1,128)S(1)} %bitcast.5), channel_id=1, replica_groups=mesh['lon_0'=8,'lon_1'=8,'lon_2'=4,'lat_0'=2,'lat_1'=2] {'lon_0','lon_1'}, dimensions={0} | all-to-all | bytes 65536 | tf_op jit(solution)/shard_map/all_to_all | solution.py:344
  62.9 0.8 %final.1 = (f32[8,512]{1,0:T(8,128)}, f32[8,512]{1,0:T(8,128)}) custom-call(f32[64,128]{1,0:T(8,128)S(1)} %bitcast.4, f32[7,8,512]{2,1,0:T(8,128)S(1)} %get-tuple-element.14.basis, f32[7,8,256]{2,1,0:T(8,128)S(1)} %get-tuple-element.15.edge_basis), custom_call_target="tpu_custom_call" | custom-call | tf_op jit(solution)/shard_map/final/pallas_call | solution.py:315
Async XLA Ops:
  2.2 26.3 %collective-permute-start = (f32[3,8,512]{2,1,0:T(8,128)S(1)}, f32[3,8,512]{2,1,0:T(8,128)S(1)}, u32[]{:S(2)}, u32[]{:S(2)}) collective-permute-start(f32[3,8,512]{2,1,0:T(8,128)S(1)} %get-tuple-element.10), channel_id=1, source_target_pairs={{0,1020},{4,8},{8,4},{12,16},{16,12},{20,24},{24,20},{28,32},{32,2... | collective-permute-start | bytes 147464 | tf_op jit(solution)/shard_map/ppermute | solution.py:338
  26.6 4.8 %collective-permute-start.1 = (f32[3,8,512]{2,1,0:T(8,128)S(1)}, f32[3,8,512]{2,1,0:T(8,128)S(1)}, u32[]{:S(2)}, u32[]{:S(2)}) collective-permute-start(f32[3,8,512]{2,1,0:T(8,128)S(1)} %get-tuple-element.11), channel_id=1, source_target_pairs={{0,4},{4,0},{8,12},{12,8},{16,20},{20,16},{24,28},{28,24},{32,36},... | collective-permute-start | bytes 147464 | tf_op jit(solution)/shard_map/ppermute | solution.py:339

commit v4 on v3

--- a/solution.py
+++ b/solution.py
@@ -17,6 +17,7 @@
 WIDTH = 7
 EDGE = 112
 MOMENTS = 122
+PLAIN = 116
 EDGE_COLS = 256
 LON = ("lon_0", "lon_1", "lon_2")
 LAT = ("lat_0", "lat_1")
@@ -109,25 +110,31 @@
 
     w0 = rhs
     v0 = w0 / diag
-    w1 = spread(v0)
+    w1 = diag * v0 - spread(v0)
     v1 = w1 / diag
-    w2 = spread(v1)
+    w2 = -spread(v1)
     v2 = w2 / diag
-    w3 = spread(v2)
+    w3 = -spread(v2)
     return [a[:ROWS] for a in (v0, v1, v2, w0, w1, w2, w3)]
 
 
-def add_moments(basis, keep, first):
-    v0, v1, v2, w0, w1, w2, w3 = basis
+def add_moments(basis, keep):
+    s0, s1, s2, w0, w1, w2, w3 = basis
+    n1, n2 = s0 - s1, s0 - s1 + s2
+    m1 = w0 - w1
+    m2 = m1 + w2
+    m3 = m2 - w3
+    plain = ((s0, m1), (n1, m1), (n1, m2), (n2, m2), (n2, m3))
+    newton = ((s0, w0), (s0, w1), (s1, w1), (s1, w2), (s2, w2), (s2, w3))
     row = jnp.zeros((1, 128), jnp.float32)
     spot = lane((1, 128))
-    for k, (a, b) in enumerate(((v0, w0), (v0, w1), (v1, w1), (v1, w2), (v2, w2), (v2, w3))):
+    for at, (a, b) in (*enumerate(plain, PLAIN), *enumerate(newton, MOMENTS)):
         prod = jnp.where(keep, a * b, 0.0)
         tiles = [prod[:, i : i + 128] for i in range(0, prod.shape[1], 128)]
         while len(tiles) > 1:
             tiles = [tiles[i] + tiles[i + 1] for i in range(0, len(tiles), 2)]
         total = jnp.sum(jnp.sum(tiles[0], axis=0, keepdims=True), axis=1, keepdims=True)
-        row = jnp.where(spot == first + k, total, row)
+        row = jnp.where(spot == at, total, row)
     return row
 
 
@@ -160,9 +167,10 @@
     low = jnp.where(place == 0, 0, REACH)
     top = jnp.where(place == lax.axis_size(LAT) - 1, COLS, COLS - REACH)
     keep = jnp.logical_and(spot >= low, spot < top)
-    row = add_moments(parts, keep, MOMENTS)
+    row = jnp.broadcast_to(add_moments(parts, keep), (ROWS, 128))
     spot = lane((ROWS, 128))
-    tile = jnp.where(sublane((ROWS, 128)) == 0, row, 0.0)
+    deep = sublane((ROWS, 128))
+    tile = jnp.where(deep == 0, row, jnp.where(deep == 1, turn(row, MOMENTS - PLAIN), 0.0))
     pieces = []
     for t in range(2):
         for i, field in enumerate((rhs, diag, face_x, face_y)):
@@ -218,12 +226,12 @@
     spot = lane((ROWS, EDGE_COLS))
     column = lax.rem(spot, 16)
     keep = jnp.logical_and(column >= WIDTH - REACH, column < WIDTH + REACH)
-    row = add_moments(parts, keep, MOMENTS)
-    total = slots[0]
-    for i in range(1, group):
-        total = total + slots[i]
-    total = total[:1] + row
-    moments[...] = jnp.broadcast_to(total, moments.shape)
+    row = add_moments(parts, keep)
+    sums = [slots[i] for i in range(group)]
+    while len(sums) > 1:
+        sums = [sums[i] + sums[i + 1] for i in range(0, len(sums), 2)]
+    total = jnp.where(lane((ROWS, 128)) >= MOMENTS, sums[0], pltpu.roll(turn(sums[0], PLAIN - MOMENTS), ROWS - 1, 0))
+    moments[...] = jnp.broadcast_to(total[:1] + row, moments.shape)
 
 
 def poly(a, b, scale):
@@ -239,46 +247,57 @@
     return out
 
 
-def dot(a, b, moments, shift=0):
+def square(a, gram):
     total = None
-    for k in range(len(a) + len(b) - 1):
-        coef = None
-        for i in range(len(a)):
-            j = k - i
-            if 0 <= j < len(b):
-                term = a[i] * b[j]
-                coef = term if coef is None else coef + term
-        term = coef * moments[k + shift]
-        total = term if total is None else total + term
+    for i in range(len(a)):
+        for j in range(i, len(a)):
+            term = a[i] * a[j] * gram[i, j]
+            term = term if i == j else 2.0 * term
+            total = term if total is None else total + term
     return total
 
 
 def final_kernel(parts, basis, edge_basis, surface, residual):
     row = jnp.sum(parts[...], axis=0, keepdims=True)
     spot = lane((1, 128))
-    moments = [jnp.sum(jnp.where(spot == MOMENTS + k, row, 0.0), axis=1, keepdims=True) for k in range(6)]
+    def at(k):
+        return jnp.sum(jnp.where(spot == k, row, 0.0), axis=1, keepdims=True)
+
+    g00, g01, g11, g12, g22, g23 = [at(MOMENTS + k) for k in range(6)]
+    m1, m2, m3, m4, m5 = [at(PLAIN + k) for k in range(5)]
+    rough = g01 > 0.5 * g00
+    newton = {(0, 0): g00, (0, 1): g01, (1, 1): g11, (0, 2): g11 - g01, (1, 2): g12, (2, 2): g22}
+    plain = {(0, 0): g00, (0, 1): m1, (1, 1): m2, (0, 2): m2, (1, 2): m3, (2, 2): m4}
+    gram = {k: jnp.where(rough, plain[k], newton[k]) for k in plain}
+    newton = {(0, 0): g01, (0, 1): g11, (1, 1): g12 + g11, (0, 2): g12, (1, 2): g22 + g12, (2, 2): g23 + g22}
+    plain = {(0, 0): g00 - m1, (0, 1): m1 - m2, (1, 1): m2 - m3, (0, 2): m2 - m3, (1, 2): m3 - m4, (2, 2): m4 - m5}
+    energy = {k: jnp.where(rough, plain[k], newton[k]) for k in plain}
+    stay, shift = jnp.where(rough, 1.0, 0.0), jnp.where(rough, -1.0, 1.0)
     one = jnp.ones((1, 1), jnp.float32)
-    gaps = [moments[k] - moments[k + 1] for k in range(5)]
-    pre = [one]
-    gamma = moments[0]
-    step = gamma / gaps[0]
-    direction = pre
+    pre, direction = [one], [one]
+    gamma = g00
+    step = gamma / energy[0, 0]
     answer = [step]
     for sweep in range(3):
-        image = [direction[0]]
-        for i in range(1, len(direction)):
-            image.append(direction[i] - direction[i - 1])
-        image.append(-direction[-1])
+        image = [stay * direction[0]]
+        for i in range(1, sweep + 1):
+            image.append(direction[i] + shift * direction[i - 1])
+        image.append(shift * direction[-1])
         pre = poly(pre, image, -step)
         if sweep == 2:
             break
-        gamma_next = dot(pre, pre, moments)
-        delta = dot(pre, pre, gaps)
+        gamma_next = square(pre, gram)
+        delta = square(pre, energy)
         ratio = gamma_next / gamma
         step = gamma_next / (delta - ratio * gamma_next / step)
         direction = poly(pre, direction, ratio)
         answer = poly(answer, direction, step)
         gamma = gamma_next
+    for coefs in (answer, pre):
+        for i in range(len(coefs) - 1, 0, -1):
+            coefs[i - 1] = coefs[i - 1] + jnp.where(rough, coefs[i], 0.0)
+        for i in range(1, len(coefs), 2):
+            coefs[i] = shift * coefs[i]
 
     def combine(b):
         eta = answer[0] * b[0] + answer[1] * b[1] + answer[2] * b[2]

time: 64 us -> 64.1 us (level)
  no operation moved by 1% of the time
where the time goes in v4:
time: 64.1 us; the launch traced here: 63.8 us
  blocking collectives  30.4 us (47%)
  starting transfers between devices  26.3 us (41%)
  Pallas kernels  3.62 us (6%)
  waiting for transfers between devices  2.9 us (5%)
  between operations  0.67 us (1%)
    ppermute x1, starting transfers between devices, body(): got_odd = lax.ppermute(odd, LON, pairs_odd)  24.3 us
    all_to_all x1, blocking collectives, body(): moments = lax.all_to_all(moments, FAR, 0, 0, tiled=True)  16.6 us
    all_to_all x1, blocking collectives, body(): slots = lax.all_to_all(slots, NEAR, 0, 0, tiled=True)  13.8 us
    ppermute x1, waiting for transfers between devices, body(): got_even = lax.ppermute(even, LON, pairs_even)  2.9 us
    pallas_call x3, Pallas kernels, call(): pl.pallas_call(kernel, out_shape=outs, in_specs=[VMEM] * len(args), out_s...  2.04 us
    ppermute x1, starting transfers between devices, body(): got_even = lax.ppermute(even, LON, pairs_even)  1.92 us
    pallas_call x1, Pallas kernels, body(): pl.pallas_call(sum_kernel, out_shape=(kept(FIELDS, ROWS, COLS), kept(3, R...  1.58 us
  transfers between devices with their start and end apart: 2, of which 1 were waited for; matrix products, arithmetic and copies ran while one was open for 0% of the time, Pallas kernels for 0%

profile of v4, /device:TPU:1, one launch (start us, length us, event | category | flops | bytes accessed | tf_op | source)
XLA Modules:
  0.0 63.8 jit_solution(2847509466522541442)
XLA Ops:
  0.6 1.6 %sums.1 = (f32[6,8,512]{2,1,0:T(8,128)S(1)}, f32[3,8,512]{2,1,0:T(8,128)S(1)}, f32[3,8,512]{2,1,0:T(8,128)S(1)}) custom-call(f32[40]{0:T(128)} %thick_in.1, f32[40,8,512]{2,1,0:T(8,128)} %u.1, f32[40,8,512]{2,1,0:T(8,128)} %v.1, f32[8,512]{1,0:T(8,128)} %depth.1, s32[8,512]{1,0:T(8,128)} %mask.1, f32[8,512]{1,0:T(8,128)} %damping.1, f32[8,512]{1,0:T(8,128)} %eta.1), custom_call_target="tpu_custom_call" | custom-call | tf_op jit(solution)/shard_map/sums/pallas_call | solution.py:341
  2.2 24.3 %collective-permute-start = (f32[3,8,512]{2,1,0:T(8,128)S(1)}, f32[3,8,512]{2,1,0:T(8,128)S(1)}, u32[]{:S(2)}, u32[]{:S(2)}) collective-permute-start(f32[3,8,512]{2,1,0:T(8,128)S(1)} %get-tuple-element.10), channel_id=1, source_target_pairs={{0,1020},{4,8},{8,4},{12,16},{16,12},{20,24},{24,20},{28,32},{32,2... | collective-permute-start | bytes 147464 | tf_op jit(solution)/shard_map/ppermute | solution.py:357
  26.6 1.9 %collective-permute-start.1 = (f32[3,8,512]{2,1,0:T(8,128)S(1)}, f32[3,8,512]{2,1,0:T(8,128)S(1)}, u32[]{:S(2)}, u32[]{:S(2)}) collective-permute-start(f32[3,8,512]{2,1,0:T(8,128)S(1)} %get-tuple-element.11), channel_id=1, source_target_pairs={{0,4},{4,0},{8,12},{12,8},{16,20},{20,16},{24,28},{28,24},{32,36},... | collective-permute-start | bytes 147464 | tf_op jit(solution)/shard_map/ppermute | solution.py:358
  28.5 0.0 collective-permute-done.got_odd
  28.5 2.9 %collective-permute-done.1.got_even = f32[3,8,512]{2,1,0:T(8,128)S(1)} collective-permute-done((f32[3,8,512]{2,1,0:T(8,128)S(1)}, f32[3,8,512]{2,1,0:T(8,128)S(1)}, u32[]{:S(2)}, u32[]{:S(2)}) %collective-permute-start.1) | collective-permute-done | bytes 49184 | tf_op jit(solution)/shard_map/ppermute | solution.py:358
  31.4 0.6 block.1
  32.0 13.8 %all_to_all.16.slots = f32[16,8,128]{2,1,0:T(8,128)S(1)} all-to-all(f32[16,8,128]{2,1,0:T(8,128)S(1)} %get-tuple-element.12), channel_id=1, replica_groups=mesh['lon_0'=8,'lon_1'=8,'lon_2'=4,'lat_0'=2,'lat_1'=2] {'lon_2','lat_0'..., dimensions={0} | all-to-all | bytes 131072 | tf_op jit(solution)/shard_map/all_to_all | solution.py:361
  45.8 0.6 %edge.1 = (f32[7,8,256]{2,1,0:T(8,128)S(1)}, f32[64,128]{1,0:T(8,128)S(1)}) custom-call(f32[16,8,128]{2,1,0:T(8,128)S(1)} %all_to_all.16.slots), custom_call_target="tpu_custom_call" | custom-call | tf_op jit(solution)/shard_map/edge/pallas_call | solution.py:334
  46.4 16.6 %all_to_all.17 = f32[64,1,128]{2,1,0:T(1,128)S(1)} all-to-all(f32[64,1,128]{2,1,0:T(1,128)S(1)} %bitcast.5), channel_id=1, replica_groups=mesh['lon_0'=8,'lon_1'=8,'lon_2'=4,'lat_0'=2,'lat_1'=2] {'lon_0','lon_1'}, dimensions={0} | all-to-all | bytes 65536 | tf_op jit(solution)/shard_map/all_to_all | solution.py:363
  63.0 0.8 %final.1 = (f32[8,512]{1,0:T(8,128)}, f32[8,512]{1,0:T(8,128)}) custom-call(f32[64,128]{1,0:T(8,128)S(1)} %bitcast.4, f32[7,8,512]{2,1,0:T(8,128)S(1)} %get-tuple-element.14.basis, f32[7,8,256]{2,1,0:T(8,128)S(1)} %get-tuple-element.15.edge_basis), custom_call_target="tpu_custom_call" | custom-call | tf_op jit(solution)/shard_map/final/pallas_call | solution.py:334
Async XLA Ops:
  2.2 26.3 %collective-permute-start = (f32[3,8,512]{2,1,0:T(8,128)S(1)}, f32[3,8,512]{2,1,0:T(8,128)S(1)}, u32[]{:S(2)}, u32[]{:S(2)}) collective-permute-start(f32[3,8,512]{2,1,0:T(8,128)S(1)} %get-tuple-element.10), channel_id=1, source_target_pairs={{0,1020},{4,8},{8,4},{12,16},{16,12},{20,24},{24,20},{28,32},{32,2... | collective-permute-start | bytes 147464 | tf_op jit(solution)/shard_map/ppermute | solution.py:357
  26.6 4.8 %collective-permute-start.1 = (f32[3,8,512]{2,1,0:T(8,128)S(1)}, f32[3,8,512]{2,1,0:T(8,128)S(1)}, u32[]{:S(2)}, u32[]{:S(2)}) collective-permute-start(f32[3,8,512]{2,1,0:T(8,128)S(1)} %get-tuple-element.11), channel_id=1, source_target_pairs={{0,4},{4,0},{8,12},{12,8},{16,20},{20,16},{24,28},{28,24},{32,36},... | collective-permute-start | bytes 147464 | tf_op jit(solution)/shard_map/ppermute | solution.py:358

commit v5 on v4

--- a/solution.py
+++ b/solution.py
@@ -9,7 +9,7 @@
 from jax.sharding import PartitionSpec as P
 
 LEVELS = 40
-CHUNKS = 4
+CHUNKS = 2
 ROWS = 8
 COLS = 512
 FIELDS = 6

time: 64.1 us -> 64 us (level)
  no operation moved by 1% of the time
where the time goes in v5:
time: 64 us; the launch traced here: 63.7 us
  blocking collectives  30.4 us (48%)
  starting transfers between devices  26.3 us (41%)
  Pallas kernels  3.49 us (5%)
  waiting for transfers between devices  2.9 us (5%)
  between operations  0.67 us (1%)
    ppermute x1, starting transfers between devices, body(): got_odd = lax.ppermute(odd, LON, pairs_odd)  24.3 us
    all_to_all x1, blocking collectives, body(): moments = lax.all_to_all(moments, FAR, 0, 0, tiled=True)  16.6 us
    all_to_all x1, blocking collectives, body(): slots = lax.all_to_all(slots, NEAR, 0, 0, tiled=True)  13.8 us
    ppermute x1, waiting for transfers between devices, body(): got_even = lax.ppermute(even, LON, pairs_even)  2.9 us
    pallas_call x3, Pallas kernels, call(): pl.pallas_call(kernel, out_shape=outs, in_specs=[VMEM] * len(args), out_s...  2.04 us
    ppermute x1, starting transfers between devices, body(): got_even = lax.ppermute(even, LON, pairs_even)  1.92 us
    pallas_call x1, Pallas kernels, body(): pl.pallas_call(sum_kernel, out_shape=(kept(FIELDS, ROWS, COLS), kept(3, R...  1.45 us
  transfers between devices with their start and end apart: 2, of which 1 were waited for; matrix products, arithmetic and copies ran while one was open for 0% of the time, Pallas kernels for 0%

profile of v5, /device:TPU:1, one launch (start us, length us, event | category | flops | bytes accessed | tf_op | source)
XLA Modules:
  0.0 63.7 jit_solution(7678845478551017050)
XLA Ops:
  0.6 1.5 %sums.1 = (f32[6,8,512]{2,1,0:T(8,128)S(1)}, f32[3,8,512]{2,1,0:T(8,128)S(1)}, f32[3,8,512]{2,1,0:T(8,128)S(1)}) custom-call(f32[40]{0:T(128)} %thick_in.1, f32[40,8,512]{2,1,0:T(8,128)} %u.1, f32[40,8,512]{2,1,0:T(8,128)} %v.1, f32[8,512]{1,0:T(8,128)} %depth.1, s32[8,512]{1,0:T(8,128)} %mask.1, f32[8,512]{1,0:T(8,128)} %damping.1, f32[8,512]{1,0:T(8,128)} %eta.1), custom_call_target="tpu_custom_call" | custom-call | tf_op jit(solution)/shard_map/sums/pallas_call | solution.py:341
  2.1 24.3 %collective-permute-start = (f32[3,8,512]{2,1,0:T(8,128)S(1)}, f32[3,8,512]{2,1,0:T(8,128)S(1)}, u32[]{:S(2)}, u32[]{:S(2)}) collective-permute-start(f32[3,8,512]{2,1,0:T(8,128)S(1)} %get-tuple-element.10), channel_id=1, source_target_pairs={{0,1020},{4,8},{8,4},{12,16},{16,12},{20,24},{24,20},{28,32},{32,2... | collective-permute-start | bytes 147464 | tf_op jit(solution)/shard_map/ppermute | solution.py:357
  26.4 1.9 %collective-permute-start.1 = (f32[3,8,512]{2,1,0:T(8,128)S(1)}, f32[3,8,512]{2,1,0:T(8,128)S(1)}, u32[]{:S(2)}, u32[]{:S(2)}) collective-permute-start(f32[3,8,512]{2,1,0:T(8,128)S(1)} %get-tuple-element.11), channel_id=1, source_target_pairs={{0,4},{4,0},{8,12},{12,8},{16,20},{20,16},{24,28},{28,24},{32,36},... | collective-permute-start | bytes 147464 | tf_op jit(solution)/shard_map/ppermute | solution.py:358
  28.4 0.0 collective-permute-done.got_odd
  28.4 2.9 %collective-permute-done.1.got_even = f32[3,8,512]{2,1,0:T(8,128)S(1)} collective-permute-done((f32[3,8,512]{2,1,0:T(8,128)S(1)}, f32[3,8,512]{2,1,0:T(8,128)S(1)}, u32[]{:S(2)}, u32[]{:S(2)}) %collective-permute-start.1) | collective-permute-done | bytes 49184 | tf_op jit(solution)/shard_map/ppermute | solution.py:358
  31.3 0.6 block.1
  31.9 13.8 %all_to_all.16.slots = f32[16,8,128]{2,1,0:T(8,128)S(1)} all-to-all(f32[16,8,128]{2,1,0:T(8,128)S(1)} %get-tuple-element.12), channel_id=1, replica_groups=mesh['lon_0'=8,'lon_1'=8,'lon_2'=4,'lat_0'=2,'lat_1'=2] {'lon_2','lat_0'..., dimensions={0} | all-to-all | bytes 131072 | tf_op jit(solution)/shard_map/all_to_all | solution.py:361
  45.6 0.6 %edge.1 = (f32[7,8,256]{2,1,0:T(8,128)S(1)}, f32[64,128]{1,0:T(8,128)S(1)}) custom-call(f32[16,8,128]{2,1,0:T(8,128)S(1)} %all_to_all.16.slots), custom_call_target="tpu_custom_call" | custom-call | tf_op jit(solution)/shard_map/edge/pallas_call | solution.py:334
  46.3 16.6 %all_to_all.17 = f32[64,1,128]{2,1,0:T(1,128)S(1)} all-to-all(f32[64,1,128]{2,1,0:T(1,128)S(1)} %bitcast.5), channel_id=1, replica_groups=mesh['lon_0'=8,'lon_1'=8,'lon_2'=4,'lat_0'=2,'lat_1'=2] {'lon_0','lon_1'}, dimensions={0} | all-to-all | bytes 65536 | tf_op jit(solution)/shard_map/all_to_all | solution.py:363
  62.9 0.8 %final.1 = (f32[8,512]{1,0:T(8,128)}, f32[8,512]{1,0:T(8,128)}) custom-call(f32[64,128]{1,0:T(8,128)S(1)} %bitcast.4, f32[7,8,512]{2,1,0:T(8,128)S(1)} %get-tuple-element.14.basis, f32[7,8,256]{2,1,0:T(8,128)S(1)} %get-tuple-element.15.edge_basis), custom_call_target="tpu_custom_call" | custom-call | tf_op jit(solution)/shard_map/final/pallas_call | solution.py:334
Async XLA Ops:
  2.1 26.3 %collective-permute-start = (f32[3,8,512]{2,1,0:T(8,128)S(1)}, f32[3,8,512]{2,1,0:T(8,128)S(1)}, u32[]{:S(2)}, u32[]{:S(2)}) collective-permute-start(f32[3,8,512]{2,1,0:T(8,128)S(1)} %get-tuple-element.10), channel_id=1, source_target_pairs={{0,1020},{4,8},{8,4},{12,16},{16,12},{20,24},{24,20},{28,32},{32,2... | collective-permute-start | bytes 147464 | tf_op jit(solution)/shard_map/ppermute | solution.py:357
  26.4 4.8 %collective-permute-start.1 = (f32[3,8,512]{2,1,0:T(8,128)S(1)}, f32[3,8,512]{2,1,0:T(8,128)S(1)}, u32[]{:S(2)}, u32[]{:S(2)}) collective-permute-start(f32[3,8,512]{2,1,0:T(8,128)S(1)} %get-tuple-element.11), channel_id=1, source_target_pairs={{0,4},{4,0},{8,12},{12,8},{16,20},{20,16},{24,28},{28,24},{32,36},... | collective-permute-start | bytes 147464 | tf_op jit(solution)/shard_map/ppermute | solution.py:358

commit v6 on v5

--- a/solution.py
+++ b/solution.py
@@ -22,7 +22,7 @@
 LON = ("lon_0", "lon_1", "lon_2")
 LAT = ("lat_0", "lat_1")
 NEAR = ("lon_2", "lat_0", "lat_1")
-FAR = ("lon_0", "lon_1")
+FAR = ("lon_1", "lon_0")
 SCALE = 1.0 / math.sqrt(LEVELS)
 VMEM = pl.BlockSpec(memory_space=pltpu.VMEM)
 ANY = pl.BlockSpec(memory_space=pl.ANY)

time: 64 us -> 64 us (level)
  no operation moved by 1% of the time
where the time goes in v6:
time: 64 us; the launch traced here: 63.7 us
  blocking collectives  30.4 us (48%)
  starting transfers between devices  26.3 us (41%)
  Pallas kernels  3.49 us (5%)
  waiting for transfers between devices  2.9 us (5%)
  between operations  0.67 us (1%)
    ppermute x1, starting transfers between devices, body(): got_odd = lax.ppermute(odd, LON, pairs_odd)  24.3 us
    all_to_all x1, blocking collectives, body(): moments = lax.all_to_all(moments, FAR, 0, 0, tiled=True)  16.6 us
    all_to_all x1, blocking collectives, body(): slots = lax.all_to_all(slots, NEAR, 0, 0, tiled=True)  13.8 us
    ppermute x1, waiting for transfers between devices, body(): got_even = lax.ppermute(even, LON, pairs_even)  2.9 us
    pallas_call x3, Pallas kernels, call(): pl.pallas_call(kernel, out_shape=outs, in_specs=[VMEM] * len(args), out_s...  2.04 us
    ppermute x1, starting transfers between devices, body(): got_even = lax.ppermute(even, LON, pairs_even)  1.92 us
    pallas_call x1, Pallas kernels, body(): pl.pallas_call(sum_kernel, out_shape=(kept(FIELDS, ROWS, COLS), kept(3, R...  1.45 us
  transfers between devices with their start and end apart: 2, of which 1 were waited for; matrix products, arithmetic and copies ran while one was open for 0% of the time, Pallas kernels for 0%

profile of v6, /device:TPU:1, one launch (start us, length us, event | category | flops | bytes accessed | tf_op | source)
XLA Modules:
  0.0 63.7 jit_solution(1072343078190704083)
XLA Ops:
  0.6 1.5 %sums.1 = (f32[6,8,512]{2,1,0:T(8,128)S(1)}, f32[3,8,512]{2,1,0:T(8,128)S(1)}, f32[3,8,512]{2,1,0:T(8,128)S(1)}) custom-call(f32[40]{0:T(128)} %thick_in.1, f32[40,8,512]{2,1,0:T(8,128)} %u.1, f32[40,8,512]{2,1,0:T(8,128)} %v.1, f32[8,512]{1,0:T(8,128)} %depth.1, s32[8,512]{1,0:T(8,128)} %mask.1, f32[8,512]{1,0:T(8,128)} %damping.1, f32[8,512]{1,0:T(8,128)} %eta.1), custom_call_target="tpu_custom_call" | custom-call | tf_op jit(solution)/shard_map/sums/pallas_call | solution.py:341
  2.1 24.3 %collective-permute-start = (f32[3,8,512]{2,1,0:T(8,128)S(1)}, f32[3,8,512]{2,1,0:T(8,128)S(1)}, u32[]{:S(2)}, u32[]{:S(2)}) collective-permute-start(f32[3,8,512]{2,1,0:T(8,128)S(1)} %get-tuple-element.10), channel_id=1, source_target_pairs={{0,1020},{4,8},{8,4},{12,16},{16,12},{20,24},{24,20},{28,32},{32,2... | collective-permute-start | bytes 147464 | tf_op jit(solution)/shard_map/ppermute | solution.py:357
  26.4 1.9 %collective-permute-start.1 = (f32[3,8,512]{2,1,0:T(8,128)S(1)}, f32[3,8,512]{2,1,0:T(8,128)S(1)}, u32[]{:S(2)}, u32[]{:S(2)}) collective-permute-start(f32[3,8,512]{2,1,0:T(8,128)S(1)} %get-tuple-element.11), channel_id=1, source_target_pairs={{0,4},{4,0},{8,12},{12,8},{16,20},{20,16},{24,28},{28,24},{32,36},... | collective-permute-start | bytes 147464 | tf_op jit(solution)/shard_map/ppermute | solution.py:358
  28.4 0.0 collective-permute-done.got_odd
  28.4 2.9 %collective-permute-done.1.got_even = f32[3,8,512]{2,1,0:T(8,128)S(1)} collective-permute-done((f32[3,8,512]{2,1,0:T(8,128)S(1)}, f32[3,8,512]{2,1,0:T(8,128)S(1)}, u32[]{:S(2)}, u32[]{:S(2)}) %collective-permute-start.1) | collective-permute-done | bytes 49184 | tf_op jit(solution)/shard_map/ppermute | solution.py:358
  31.3 0.6 block.1
  31.9 13.8 %all_to_all.16.slots = f32[16,8,128]{2,1,0:T(8,128)S(1)} all-to-all(f32[16,8,128]{2,1,0:T(8,128)S(1)} %get-tuple-element.12), channel_id=1, replica_groups=mesh['lon_0'=8,'lon_1'=8,'lon_2'=4,'lat_0'=2,'lat_1'=2] {'lon_2','lat_0'..., dimensions={0} | all-to-all | bytes 131072 | tf_op jit(solution)/shard_map/all_to_all | solution.py:361
  45.6 0.6 %edge.1 = (f32[7,8,256]{2,1,0:T(8,128)S(1)}, f32[64,128]{1,0:T(8,128)S(1)}) custom-call(f32[16,8,128]{2,1,0:T(8,128)S(1)} %all_to_all.16.slots), custom_call_target="tpu_custom_call" | custom-call | tf_op jit(solution)/shard_map/edge/pallas_call | solution.py:334
  46.3 16.6 %all_to_all.17 = f32[64,1,128]{2,1,0:T(1,128)S(1)} all-to-all(f32[64,1,128]{2,1,0:T(1,128)S(1)} %bitcast.5), channel_id=1, replica_groups=mesh['lon_0'=8,'lon_1'=8,'lon_2'=4,'lat_0'=2,'lat_1'=2] {'lon_1','lon_0'}, dimensions={0} | all-to-all | bytes 65536 | tf_op jit(solution)/shard_map/all_to_all | solution.py:363
  62.9 0.8 %final.1 = (f32[8,512]{1,0:T(8,128)}, f32[8,512]{1,0:T(8,128)}) custom-call(f32[64,128]{1,0:T(8,128)S(1)} %bitcast.4, f32[7,8,512]{2,1,0:T(8,128)S(1)} %get-tuple-element.14.basis, f32[7,8,256]{2,1,0:T(8,128)S(1)} %get-tuple-element.15.edge_basis), custom_call_target="tpu_custom_call" | custom-call | tf_op jit(solution)/shard_map/final/pallas_call | solution.py:334
Async XLA Ops:
  2.1 26.3 %collective-permute-start = (f32[3,8,512]{2,1,0:T(8,128)S(1)}, f32[3,8,512]{2,1,0:T(8,128)S(1)}, u32[]{:S(2)}, u32[]{:S(2)}) collective-permute-start(f32[3,8,512]{2,1,0:T(8,128)S(1)} %get-tuple-element.10), channel_id=1, source_target_pairs={{0,1020},{4,8},{8,4},{12,16},{16,12},{20,24},{24,20},{28,32},{32,2... | collective-permute-start | bytes 147464 | tf_op jit(solution)/shard_map/ppermute | solution.py:357
  26.4 4.8 %collective-permute-start.1 = (f32[3,8,512]{2,1,0:T(8,128)S(1)}, f32[3,8,512]{2,1,0:T(8,128)S(1)}, u32[]{:S(2)}, u32[]{:S(2)}) collective-permute-start(f32[3,8,512]{2,1,0:T(8,128)S(1)} %get-tuple-element.11), channel_id=1, source_target_pairs={{0,4},{4,0},{8,12},{12,8},{16,20},{20,16},{24,28},{28,24},{32,36},... | collective-permute-start | bytes 147464 | tf_op jit(solution)/shard_map/ppermute | solution.py:358

commit v7 on v5

--- a/solution.py
+++ b/solution.py
@@ -9,7 +9,7 @@
 from jax.sharding import PartitionSpec as P
 
 LEVELS = 40
-CHUNKS = 2
+CHUNKS = 1
 ROWS = 8
 COLS = 512
 FIELDS = 6

time: 64 us -> 64 us (level)
  no operation moved by 1% of the time
where the time goes in v7:
time: 64 us; the launch traced here: 63.7 us
  blocking collectives  30.4 us (48%)
  starting transfers between devices  26.3 us (41%)
  Pallas kernels  3.52 us (6%)
  waiting for transfers between devices  2.9 us (5%)
  between operations  0.67 us (1%)
    ppermute x1, starting transfers between devices, body(): got_odd = lax.ppermute(odd, LON, pairs_odd)  24.3 us
    all_to_all x1, blocking collectives, body(): moments = lax.all_to_all(moments, FAR, 0, 0, tiled=True)  16.6 us
    all_to_all x1, blocking collectives, body(): slots = lax.all_to_all(slots, NEAR, 0, 0, tiled=True)  13.8 us
    ppermute x1, waiting for transfers between devices, body(): got_even = lax.ppermute(even, LON, pairs_even)  2.9 us
    pallas_call x3, Pallas kernels, call(): pl.pallas_call(kernel, out_shape=outs, in_specs=[VMEM] * len(args), out_s...  2.04 us
    ppermute x1, starting transfers between devices, body(): got_even = lax.ppermute(even, LON, pairs_even)  1.92 us
    pallas_call x1, Pallas kernels, body(): pl.pallas_call(sum_kernel, out_shape=(kept(FIELDS, ROWS, COLS), kept(3, R...  1.47 us
  transfers between devices with their start and end apart: 2, of which 1 were waited for; matrix products, arithmetic and copies ran while one was open for 0% of the time, Pallas kernels for 0%

profile of v7, /device:TPU:1, one launch (start us, length us, event | category | flops | bytes accessed | tf_op | source)
XLA Modules:
  0.0 63.7 jit_solution(1795876726233736837)
XLA Ops:
  0.6 1.5 %sums.1 = (f32[6,8,512]{2,1,0:T(8,128)S(1)}, f32[3,8,512]{2,1,0:T(8,128)S(1)}, f32[3,8,512]{2,1,0:T(8,128)S(1)}) custom-call(f32[40]{0:T(128)} %thick_in.1, f32[40,8,512]{2,1,0:T(8,128)} %u.1, f32[40,8,512]{2,1,0:T(8,128)} %v.1, f32[8,512]{1,0:T(8,128)} %depth.1, s32[8,512]{1,0:T(8,128)} %mask.1, f32[8,512]{1,0:T(8,128)} %damping.1, f32[8,512]{1,0:T(8,128)} %eta.1), custom_call_target="tpu_custom_call" | custom-call | tf_op jit(solution)/shard_map/sums/pallas_call | solution.py:341
  2.1 24.3 %collective-permute-start = (f32[3,8,512]{2,1,0:T(8,128)S(1)}, f32[3,8,512]{2,1,0:T(8,128)S(1)}, u32[]{:S(2)}, u32[]{:S(2)}) collective-permute-start(f32[3,8,512]{2,1,0:T(8,128)S(1)} %get-tuple-element.10), channel_id=1, source_target_pairs={{0,1020},{4,8},{8,4},{12,16},{16,12},{20,24},{24,20},{28,32},{32,2... | collective-permute-start | bytes 147464 | tf_op jit(solution)/shard_map/ppermute | solution.py:357
  26.5 1.9 %collective-permute-start.1 = (f32[3,8,512]{2,1,0:T(8,128)S(1)}, f32[3,8,512]{2,1,0:T(8,128)S(1)}, u32[]{:S(2)}, u32[]{:S(2)}) collective-permute-start(f32[3,8,512]{2,1,0:T(8,128)S(1)} %get-tuple-element.11), channel_id=1, source_target_pairs={{0,4},{4,0},{8,12},{12,8},{16,20},{20,16},{24,28},{28,24},{32,36},... | collective-permute-start | bytes 147464 | tf_op jit(solution)/shard_map/ppermute | solution.py:358
  28.4 0.0 collective-permute-done.got_odd
  28.4 2.9 %collective-permute-done.1.got_even = f32[3,8,512]{2,1,0:T(8,128)S(1)} collective-permute-done((f32[3,8,512]{2,1,0:T(8,128)S(1)}, f32[3,8,512]{2,1,0:T(8,128)S(1)}, u32[]{:S(2)}, u32[]{:S(2)}) %collective-permute-start.1) | collective-permute-done | bytes 49184 | tf_op jit(solution)/shard_map/ppermute | solution.py:358
  31.3 0.6 block.1
  31.9 13.8 %all_to_all.16.slots = f32[16,8,128]{2,1,0:T(8,128)S(1)} all-to-all(f32[16,8,128]{2,1,0:T(8,128)S(1)} %get-tuple-element.12), channel_id=1, replica_groups=mesh['lon_0'=8,'lon_1'=8,'lon_2'=4,'lat_0'=2,'lat_1'=2] {'lon_2','lat_0'..., dimensions={0} | all-to-all | bytes 131072 | tf_op jit(solution)/shard_map/all_to_all | solution.py:361
  45.7 0.6 %edge.1 = (f32[7,8,256]{2,1,0:T(8,128)S(1)}, f32[64,128]{1,0:T(8,128)S(1)}) custom-call(f32[16,8,128]{2,1,0:T(8,128)S(1)} %all_to_all.16.slots), custom_call_target="tpu_custom_call" | custom-call | tf_op jit(solution)/shard_map/edge/pallas_call | solution.py:334
  46.3 16.6 %all_to_all.17 = f32[64,1,128]{2,1,0:T(1,128)S(1)} all-to-all(f32[64,1,128]{2,1,0:T(1,128)S(1)} %bitcast.5), channel_id=1, replica_groups=mesh['lon_0'=8,'lon_1'=8,'lon_2'=4,'lat_0'=2,'lat_1'=2] {'lon_0','lon_1'}, dimensions={0} | all-to-all | bytes 65536 | tf_op jit(solution)/shard_map/all_to_all | solution.py:363
  62.9 0.8 %final.1 = (f32[8,512]{1,0:T(8,128)}, f32[8,512]{1,0:T(8,128)}) custom-call(f32[64,128]{1,0:T(8,128)S(1)} %bitcast.4, f32[7,8,512]{2,1,0:T(8,128)S(1)} %get-tuple-element.14.basis, f32[7,8,256]{2,1,0:T(8,128)S(1)} %get-tuple-element.15.edge_basis), custom_call_target="tpu_custom_call" | custom-call | tf_op jit(solution)/shard_map/final/pallas_call | solution.py:334
Async XLA Ops:
  2.1 26.3 %collective-permute-start = (f32[3,8,512]{2,1,0:T(8,128)S(1)}, f32[3,8,512]{2,1,0:T(8,128)S(1)}, u32[]{:S(2)}, u32[]{:S(2)}) collective-permute-start(f32[3,8,512]{2,1,0:T(8,128)S(1)} %get-tuple-element.10), channel_id=1, source_target_pairs={{0,1020},{4,8},{8,4},{12,16},{16,12},{20,24},{24,20},{28,32},{32,2... | collective-permute-start | bytes 147464 | tf_op jit(solution)/shard_map/ppermute | solution.py:357
  26.5 4.8 %collective-permute-start.1 = (f32[3,8,512]{2,1,0:T(8,128)S(1)}, f32[3,8,512]{2,1,0:T(8,128)S(1)}, u32[]{:S(2)}, u32[]{:S(2)}) collective-permute-start(f32[3,8,512]{2,1,0:T(8,128)S(1)} %get-tuple-element.11), channel_id=1, source_target_pairs={{0,4},{4,0},{8,12},{12,8},{16,20},{20,16},{24,28},{28,24},{32,36},... | collective-permute-start | bytes 147464 | tf_op jit(solution)/shard_map/ppermute | solution.py:358
